TPU v7x, 32 devices: a whole 2x2x4 slice. The times are simulated.
32 devices in a mesh: row: 8 (over y, x, core), col: 4 (over z).
Axes of the slice: x: 2, y: 2, z: 4, core: 2. Of those that a mesh axis runs over, the one named last changes fastest.
Arguments:
- surface_height: float32 [2048, 2048], P('row', 'col'), may hold values from -1.2 to 1.2
- surface_potential: float32 [2048, 2048], P('row', 'col'), may hold values from -4 to 4
- velocity: float32 [3, 16, 1024, 1024], P(None, None, 'row', 'col'), may hold values from -1.25 to 1.25
Outputs:
- height_rate: float32 [2048, 2048], P('row', 'col')
- potential_rate: float32 [2048, 2048], P('row', 'col')
- velocity_next: float32 [3, 16, 1024, 1024], P(None, None, 'row', 'col')
All inputs are finite; a program needn't handle non-finite values.
Results may differ from a plain program's by a relative error of at most 0.00019.
Values sent between devices are 32-bit elements; how exact they have to be, the bound alone decides.
No kernel may reach another device: no remote copies, remote signals or barrier semaphores. Data moves between devices by JAX's collectives and lax.ppermute only.
A program may use at most 192 MiB of HBM per device.

v0:
```python
import jax
import jax.numpy as jnp
from jax import lax
from jax.sharding import PartitionSpec as P

NX = 2048
NY = 2048
COARSE = 2


GRAVITY = 1.0
SURFACE_STEP = 0.05
FLOW_STEP = 0.5
VISCOSITY = 0.2
DECAY_RATE = 0.05


def with_halo(x, sides, width):
    for axis, dim in sides:
        peers, length = (lax.axis_size(axis), x.shape[dim])
        up = [(i, (i + 1) % peers) for i in range(peers)]
        down = [(j, i) for i, j in up]
        last = lax.slice_in_dim(x, length - width, length, axis=dim)
        leading = lax.slice_in_dim(x, 0, width, axis=dim)
        before = lax.ppermute(last, axis, up)
        after = lax.ppermute(leading, axis, down)
        x = jnp.concatenate([before, x, after], axis=dim)
    return x


def wave_numbers(index, length):
    signed = jnp.where(index < length // 2, index, index - length)
    kept_mask = (jnp.abs(signed) <= length // 3).astype(jnp.float32)
    return (2.0 * jnp.pi / length * signed.astype(jnp.float32), kept_mask)


def coarsen(source):
    rows_out = source.shape[0] // COARSE
    cols_out = source.shape[1] // COARSE
    return source.reshape(rows_out, COARSE, cols_out, COARSE).mean(axis=(1, 3))


def flow_update(padded_flow, padded_load, surface_u, surface_v):
    depth_count = padded_flow.shape[1]
    level_mid = jnp.arange(depth_count, dtype=jnp.float32)[:, None, None] + 0.5
    drift_decay = jnp.exp(-2.0 * DECAY_RATE * level_mid)
    load_decay = jnp.exp(-DECAY_RATE * level_mid)

    def derivs(source, top_value):
        middle = source[:, 1:-1, 1:-1]
        above_cell = jnp.concatenate([top_value[None], middle[:-1]], axis=0)
        below_cell = jnp.concatenate([middle[1:], middle[-1:]], axis=0)
        east_side = source[:, 1:-1, 2:]
        west_side = source[:, 1:-1, :-2]
        north_side = source[:, 2:, 1:-1]
        south_side = source[:, :-2, 1:-1]
        laplace = (
            east_side + west_side + north_side + south_side + above_cell + below_cell - 6.0 * middle
        )
        return (
            middle,
            0.5 * (east_side - west_side),
            0.5 * (north_side - south_side),
            0.5 * (above_cell - below_cell),
            laplace,
        )

    u_mid, u_dx, u_dy, u_dz, u_lap = derivs(padded_flow[0], surface_u)
    v_mid, v_dx, v_dy, v_dz, v_lap = derivs(padded_flow[1], surface_v)
    w_mid, w_dx, w_dy, w_dz, w_lap = derivs(padded_flow[2], jnp.zeros_like(surface_u))
    vort_x = w_dy - v_dz
    vort_y = u_dz - w_dx
    vort_z = v_dx - u_dy
    drift_u = surface_u[None] * drift_decay
    drift_v = surface_v[None] * drift_decay
    load_x = 0.5 * (padded_load[1:-1, 2:] - padded_load[1:-1, :-2])[None] * load_decay
    load_y = 0.5 * (padded_load[2:, 1:-1] - padded_load[:-2, 1:-1])[None] * load_decay

    def advance(middle, slope_x, slope_y, slope_z, laplace, forcing):
        carried = u_mid * slope_x + v_mid * slope_y + w_mid * slope_z
        return middle + FLOW_STEP * (-carried + VISCOSITY * laplace + forcing)

    next_u = advance(u_mid, u_dx, u_dy, u_dz, u_lap, drift_v * vort_z - load_x)
    next_v = advance(v_mid, v_dx, v_dy, v_dz, v_lap, -drift_u * vort_z - load_y)
    next_w = advance(w_mid, w_dx, w_dy, w_dz, w_lap, drift_u * vort_y - drift_v * vort_x)
    return jnp.stack([next_u, next_v, next_w])


def product(form, left, right):
    return jnp.einsum(form, left, right, precision=lax.Precision.HIGHEST)


def complex_product(form, left_real, left_imag, right_real, right_imag):
    if left_imag is None:
        return (product(form, left_real, right_real), product(form, left_real, right_imag))
    out_real = product(form, left_real, right_real) - product(form, left_imag, right_imag)
    out_imag = product(form, left_real, right_imag) + product(form, left_imag, right_real)
    return (out_real, out_imag)


def tables(length, direction):
    index = jnp.arange(length, dtype=jnp.int32)
    angle = 2.0 * jnp.pi / length * (index[:, None] * index[None, :] % length).astype(jnp.float32)
    return (jnp.cos(angle), direction * jnp.sin(angle))


def twiddles(factor_one, factor_two, direction):
    total = factor_one * factor_two
    index_one = jnp.arange(factor_one, dtype=jnp.int32)
    index_two = jnp.arange(factor_two, dtype=jnp.int32)
    angle = (
        2.0 * jnp.pi / total * (index_one[:, None] * index_two[None, :] % total).astype(jnp.float32)
    )
    return (jnp.cos(angle), direction * jnp.sin(angle))


def transform(real_part, imag_part, direction, layout, real_only):
    if layout == "back":
        length = real_part.shape[1]
    else:
        length = real_part.shape[2]
    factor_one = 1 << (length.bit_length() - 1) // 2
    factor_two = length // factor_one
    cos_one, sin_one = tables(factor_one, direction)
    cos_two, sin_two = tables(factor_two, direction)
    twist_cos, twist_sin = twiddles(factor_one, factor_two, direction)
    batch_size = real_part.shape[0]
    if layout == "back":
        cross_len = real_part.shape[2]
        shape_four = (batch_size, factor_one, factor_two, cross_len)
        first_form = "banm,ak->bknm"
        second_form = "bknm,nq->bmqk"
        twist_cos = twist_cos[None, :, :, None]
        twist_sin = twist_sin[None, :, :, None]
        out_shape = (batch_size, cross_len, length)
    else:
        cross_len = real_part.shape[1]
        shape_four = (batch_size, cross_len, factor_one, factor_two)
        first_form = "bman,ak->bmkn"
        twist_cos = twist_cos[None, None]
        twist_sin = twist_sin[None, None]
        if layout == "front":
            second_form = "bmkn,nq->bqkm"
            out_shape = (batch_size, length, cross_len)
        else:
            second_form = "bmkn,nq->bmqk"
            out_shape = (batch_size, cross_len, length)
    left_real = real_part.reshape(shape_four)
    left_imag = None if imag_part is None else imag_part.reshape(shape_four)
    mid_real, mid_imag = complex_product(first_form, left_real, left_imag, cos_one, sin_one)
    turned_real = mid_real * twist_cos - mid_imag * twist_sin
    turned_imag = mid_real * twist_sin + mid_imag * twist_cos
    if real_only:
        result = product(second_form, turned_real, cos_two) - product(
            second_form, turned_imag, sin_two
        )
        return result.reshape(out_shape)
    out_real, out_imag = complex_product(second_form, turned_real, turned_imag, cos_two, sin_two)
    return (out_real.reshape(out_shape), out_imag.reshape(out_shape))


def scaled(pair_value, factor):
    return (pair_value[0] * factor, pair_value[1] * factor)


def turned(pair_value, factor):
    return (-factor * pair_value[1], factor * pair_value[0])


def unfold_half(full_real, full_imag, kept_modes):
    weights = jnp.where(jnp.arange(kept_modes, dtype=jnp.int32) == 0, 1.0, 2.0).astype(jnp.float32)[
        None, :, None
    ]
    padding = jnp.zeros((full_real.shape[0], NX - kept_modes, full_real.shape[2]), jnp.float32)
    return (
        jnp.concatenate([full_real * weights, padding], axis=1),
        jnp.concatenate([full_imag * weights, padding], axis=1),
    )


def local(surface_height, surface_potential, velocity):
    col_count = lax.axis_size("col")
    device_count = lax.axis_size("row") * col_count
    place = lax.axis_index("row") * col_count + lax.axis_index("col")
    kept_modes = (NX // 3 + device_count) // device_count * device_count
    modes_each = kept_modes // device_count
    kx_index = place * modes_each + jnp.arange(modes_each, dtype=jnp.int32)
    kx_values, kx_kept = wave_numbers(kx_index, NX)
    ky_values, ky_kept = wave_numbers(jnp.arange(NY, dtype=jnp.int32), NY)
    kx_grid = kx_values[:, None]
    ky_grid = ky_values[None, :]
    mask = kx_kept[:, None] * ky_kept[None, :]
    magnitude = jnp.sqrt(kx_grid * kx_grid + ky_grid * ky_grid)

    def forward(stacked):
        pencil = lax.all_to_all(stacked, "col", split_axis=1, concat_axis=2, tiled=True)
        wide_real, wide_imag = transform(pencil, None, -1.0, "front", False)
        slab_real, slab_imag = (
            lax.all_to_all(
                wide_real[:, :kept_modes], ("row", "col"), split_axis=1, concat_axis=2, tiled=True
            ),
            lax.all_to_all(
                wide_imag[:, :kept_modes], ("row", "col"), split_axis=1, concat_axis=2, tiled=True
            ),
        )
        spec_real, spec_imag = transform(slab_real, slab_imag, -1.0, "last", False)
        return (spec_real * mask, spec_imag * mask)

    def inverse(pair_list):
        spec_real = jnp.stack([pair_item[0] for pair_item in pair_list])
        spec_imag = jnp.stack([pair_item[1] for pair_item in pair_list])
        line_real, line_imag = transform(spec_real, spec_imag, 1.0, "last", False)
        full_real, full_imag = (
            lax.all_to_all(line_real, ("row", "col"), split_axis=2, concat_axis=1, tiled=True),
            lax.all_to_all(line_imag, ("row", "col"), split_axis=2, concat_axis=1, tiled=True),
        )
        full_real, full_imag = unfold_half(full_real, full_imag, kept_modes)
        pencil = transform(full_real, full_imag, 1.0, "back", True) / float(NX * NY)
        return lax.all_to_all(pencil, "col", split_axis=2, concat_axis=1, tiled=True)

    first_real, first_imag = forward(jnp.stack([surface_potential, surface_height]))
    pot_hat = (first_real[0], first_imag[0])
    height_hat = (first_real[1], first_imag[1])
    first_fields = inverse(
        [
            scaled(pot_hat, magnitude),
            scaled(pot_hat, magnitude * magnitude),
            scaled(pot_hat, magnitude * magnitude * magnitude),
            turned(pot_hat, kx_grid),
            turned(pot_hat, ky_grid),
            turned(height_hat, kx_grid),
            turned(height_hat, ky_grid),
        ]
    )
    vert_one = first_fields[0]
    curve_one = first_fields[1]
    cube_one = first_fields[2]
    pot_dx = first_fields[3]
    pot_dy = first_fields[4]
    height_dx = first_fields[5]
    height_dy = first_fields[6]
    second_pot = -surface_height * vert_one
    second_real, second_imag = forward(second_pot[None])
    second_hat = (second_real[0], second_imag[0])
    second_fields = inverse(
        [scaled(second_hat, magnitude), scaled(second_hat, magnitude * magnitude)]
    )
    vert_two = second_fields[0]
    curve_two = second_fields[1]
    third_pot = -surface_height * vert_two - 0.5 * surface_height * surface_height * curve_one
    third_real, third_imag = forward(third_pot[None])
    vert_three = inverse([scaled((third_real[0], third_imag[0]), magnitude)])[0]
    vertical = (
        vert_one
        + vert_two
        + vert_three
        + surface_height * (curve_one + curve_two)
        + 0.5 * surface_height * surface_height * cube_one
    )
    slope = height_dx * height_dx + height_dy * height_dy
    height_rate = -(height_dx * pot_dx + height_dy * pot_dy) + (1.0 + slope) * vertical
    potential_rate = (
        -GRAVITY * surface_height
        - 0.5 * (pot_dx * pot_dx + pot_dy * pot_dy)
        + 0.5 * (1.0 + slope) * vertical * vertical
    )
    pressure = GRAVITY * coarsen(surface_height + SURFACE_STEP * height_rate)
    surface_u = coarsen(pot_dx)
    surface_v = coarsen(pot_dy)
    depth_count = velocity.shape[1]
    stacked_block = jnp.concatenate(
        [velocity.reshape((3 * depth_count,) + velocity.shape[2:]), pressure[None]], axis=0
    )
    padded_block = with_halo(stacked_block, (("row", 1), ("col", 2)), 1)
    padded_flow = padded_block[:-1].reshape((3, depth_count) + padded_block.shape[1:])
    padded_load = padded_block[-1]
    velocity_next = flow_update(padded_flow, padded_load, surface_u, surface_v)
    return (height_rate, potential_rate, velocity_next)


def solution(mesh):
    placed = (P("row", "col"), P("row", "col"), P(None, None, "row", "col"))
    return jax.shard_map(
        local,
        mesh=mesh,
        in_specs=placed,
        out_specs=(P("row", "col"), P("row", "col"), P(None, None, "row", "col")),
        check_vma=False,
    )
```

profile of v0, /device:TPU:3, one launch (start us, length us, event | category | flops | bytes accessed | tf_op | source)
XLA Modules:
  0.0 1154.4 jit_solution(16676131962339563223)
XLA Ops:
  10.2 25.0 %all-to-all-done = f32[2,256,512]{2,0,1:T(2,128)S(1)} async-done(((f32[2,256,512]{2,0,1:T(2,128)}), f32[2,256,512]{2,0,1:T(2,128)S(1)}, u32[]{:S(2)}, u32[]{:S(2)}) %all-to-all-start) | async-done | bytes 1048608 | tf_op jit(solution)/shard_map/all_to_all | solution.py:196
  51.8 18.9 %subtract_bitcast_fusion.3 = f32[2,64,32,64]{3,1,2,0:T(8,128)S(1)} fusion(f32[64,2,64,32]{2,0,3,1:T(8,128)S(1)} %fusion.71, f32[2,64,32,64]{3,2,1,0:T(8,128)S(1)} %get-tuple-element.49), kind=kOutput, calls=%fused_computation.117 | convolution fusion | flops 201646080 | bytes 3145728 | tf_op jit(solution)/shard_map/bmkn,nq->bqkm/dot_general | solution.py:90
  134.1 9.1 multiply_reduce_fusion.4
  183.2 8.6 copy.815
  211.9 8.6 copy.820
  258.2 10.3 all-to-all-done.4
  294.5 14.8 %fusion.4 = f32[32,7,64,64]{3,0,2,1:T(8,128)} fusion(f32[7,32,64,64]{3,2,1,0:T(8,128)S(1)} %bitcast.784), kind=kOutput, calls=%fused_computation.7 | convolution fusion | flops 352335872 | bytes 7340032 | tf_op jit(solution)/shard_map/banm,ak->bknm/dot_general | solution.py:90
  309.3 14.9 %fusion.6 = f32[32,7,64,64]{3,0,2,1:T(8,128)} fusion(f32[7,32,64,64]{3,2,1,0:T(8,128)S(1)} %bitcast.785), kind=kOutput, calls=%fused_computation.9 | convolution fusion | flops 352335872 | bytes 7340032 | tf_op jit(solution)/shard_map/banm,ak->bknm/dot_general | solution.py:90
  324.7 15.1 %fusion.8 = f32[32,7,64,64]{3,0,2,1:T(8,128)} fusion(f32[7,32,64,64]{3,2,1,0:T(8,128)S(1)} %bitcast.786), kind=kOutput, calls=%fused_computation.11 | convolution fusion | flops 352335872 | bytes 7340032 | tf_op jit(solution)/shard_map/banm,ak->bknm/dot_general | solution.py:90
  339.8 22.3 %subtract_bitcast_fusion = (f32[7,32,64,64]{3,1,2,0:T(8,128)}, f32[7,32,64,64]{3,1,2,0:T(8,128)}) fusion(f32[32,64]{0,1:T(8,128)S(1)} %copy.677, f32[32,64]{0,1:T(8,128)S(1)} %copy.674, f32[32,7,64,64]{3,0,2,1:T(8,128)} %fusion.8, f32[32,7,64,64]{3,0,2,1:T(8,128)} %fusion.4, f32[32,7,64,64]{3,0,2,1:T(8,128)} %fusion.6, f32[7,32,64,64]{3,2,1,0:T(8,128)S(1)} %bitcast.787), kind=kOutput, calls=%fused_computation.6 | convolution fusion | flops 359675904 | bytes 22036480 | tf_op jit(solution)/shard_map/banm,ak->bknm/dot_general | solution.py:90
  362.2 12.5 %fusion = f32[64,7,32,64]{3,0,2,1:T(8,128)S(1)} fusion(f32[7,32,64,64]{3,1,2,0:T(8,128)} %get-tuple-element.33), kind=kOutput, calls=%fused_computation | convolution fusion | flops 704700416 | bytes 7340032 | tf_op jit(solution)/shard_map/bknm,nq->bmqk/dot_general | solution.py:90
  374.7 11.4 multiply_bitcast_fusion
  390.7 12.8 %copy.1009 = f32[7,64,2048]{1,0,2:T(8,128)} copy(f32[7,64,2048]{1,2,0:T(8,128)S(1)} %bitcast.794) | data formatting | bytes 7340032 | tf_op jit(solution)/shard_map/div | solution.py:218
  411.7 87.1 %all_to_all.288 = f32[4,1,229376]{2,1,0:T(1,128)} all-to-all(f32[4,1,229376]{2,1,0:T(1,128)} %reshape.1239), channel_id=1, replica_groups=mesh['row'=8,'col'=4] {'col'}, dimensions={0} | all-to-all | bytes 7340032 | tf_op jit(solution)/shard_map/all_to_all | solution.py:219
  498.8 13.7 %reduce.32 = f32[4,229376]{1,0:T(4,128)} reduce(f32[4,1,229376]{2,1,0:T(1,128)} %all_to_all.288, f32[]{:T(128)} %broadcast.1607), dimensions={1}, to_apply=%all_to_all.227.reduce_sub_computation | reduce | bytes 7340036 | tf_op jit(solution)/shard_map/all_to_all | solution.py:219
  512.5 9.0 reshape.1240
  537.1 14.6 %all-to-all-done.6 = f32[1,256,512]{2,0,1:T(1,128)S(1)} async-done(((f32[1,256,512]{2,0,1:T(1,128)}), f32[1,256,512]{2,0,1:T(1,128)S(1)}, u32[]{:S(2)}, u32[]{:S(2)}) %all-to-all-start.6) | async-done | bytes 524320 | tf_op jit(solution)/shard_map/all_to_all | solution.py:196
  704.3 28.6 %all_to_all.289 = f32[4,1,65536]{2,1,0:T(1,128)} all-to-all(f32[4,1,65536]{2,1,0:T(1,128)S(1)} %reshape.1249), channel_id=1, replica_groups=mesh['row'=8,'col'=4] {'col'}, dimensions={0} | all-to-all | bytes 2097152 | tf_op jit(solution)/shard_map/all_to_all | solution.py:219
  745.3 16.1 %all_to_all.290 = f32[1,256,512]{2,0,1:T(1,128)S(1)} all-to-all(f32[1,256,512]{2,0,1:T(1,128)S(1)} %copy.728), channel_id=1, replica_groups=mesh['row'=8,'col'=4] {'col'}, dimensions={1} | all-to-all | bytes 1048576 | tf_op jit(solution)/shard_map/all_to_all | solution.py:196
  822.5 10.6 reduce.46
  841.1 10.4 reduce.44
  890.3 10.6 reduce.48
  905.8 9.0 fusion.811
  914.8 34.8 %reshape_squeeze.7 = f32[128,2,256,2]{3,2,1,0:T(8,128)} reshape(f32[1,4,64,512]{3,2,1,0:T(8,128)S(1)} %copy-done.25) | data formatting | bytes 1048576 | tf_op jit(solution)/shard_map/reshape;squeeze | solution.py:40
  949.7 13.3 %reduce_sum.29 = f32[128,256]{1,0:T(8,128)S(1)} reduce(f32[128,2,256,2]{3,2,1,0:T(8,128)} %reshape_squeeze.7, f32[]{:T(128)} %constant.215.clone.1), dimensions={1,3}, to_apply=%region_2.3 | reduce | flops 98304 | bytes 655364 | tf_op jit(solution)/shard_map/reduce_sum | solution.py:40
  963.0 34.9 %reshape_squeeze.6 = f32[128,2,256,2]{3,2,1,0:T(8,128)} reshape(f32[1,4,64,512]{3,2,1,0:T(8,128)S(1)} %copy-done.24) | data formatting | bytes 1048576 | tf_op jit(solution)/shard_map/reshape;squeeze | solution.py:40
  997.8 13.3 %reduce_sum.28 = f32[128,256]{1,0:T(8,128)S(1)} reduce(f32[128,2,256,2]{3,2,1,0:T(8,128)} %reshape_squeeze.6, f32[]{:T(128)} %constant.215.clone.1), dimensions={1,3}, to_apply=%region_1.2 | reduce | flops 98304 | bytes 655364 | tf_op jit(solution)/shard_map/reduce_sum | solution.py:40
  1025.7 35.6 %reshape.1180 = f32[128,2,256,2]{3,2,1,0:T(8,128)} reshape(f32[256,512]{1,0:T(8,128)} %get-tuple-element.29) | data formatting | bytes 1048576 | tf_op jit(solution)/shard_map/reshape | solution.py:40
  1061.3 13.2 %reduce_sum.27 = f32[128,256]{1,0:T(8,128)S(1)} reduce(f32[128,2,256,2]{3,2,1,0:T(8,128)} %reshape.1180, f32[]{:T(128)} %constant.215.clone.1), dimensions={1,3}, to_apply=%region_0.1 | reduce | flops 98304 | bytes 655364 | tf_op jit(solution)/shard_map/reduce_sum | solution.py:40
  1112.5 12.8 %fusion.26 = f32[1,16,128,256]{3,2,1,0:T(8,128)} fusion(f32[49,1,256]{2,1,0:T(1,128)S(1)} %copy-done.32, f32[1,128,256]{2,1,0:T(8,128)S(1)} %multiply_bitcast_fusion.2, f32[48,128,256]{2,1,0:T(8,128)S(1)} %bitcast.781, f32[49,1,256]{2,1,0:T(1,128)S(1)} %copy-done.30, f32[49,130,1]{2,1,0:T(8,128)S(1)} %copy-done, f32[49,130,1]{2,1,0:T(8,128)S(1)} %copy-done.1, ...), kind=kLoop, calls=%fused_computation.37 | loop fusion | flops 27787264 | bytes 19419024 | tf_op jit(solution)/shard_map/stack | solution.py:86
  1125.3 11.0 fusion.37
  1136.4 11.5 fusion.31
  (406 shorter events, 577.0 us)
Async XLA Ops:
  5.4 29.9 %all-to-all-start = ((f32[2,256,512]{2,0,1:T(2,128)}), f32[2,256,512]{2,0,1:T(2,128)S(1)}, u32[]{:S(2)}, u32[]{:S(2)}) async-start(f32[2,256,512]{2,0,1:T(2,128)} %pad_maximum_fusion.27), calls=%async_computation | async-start | bytes 2097152 | tf_op jit(solution)/shard_map/all_to_all | solution.py:196
  10.0 29.1 %copy-start.49 = (f32[22]{0:T(128)}, f32[22]{0:T(128)S(1)}, u32[]{:S(2)}) copy-start(f32[22]{0:T(128)S(1)} %compare_convert_fusion) | copy-start | bytes 268
  76.0 23.9 %all-to-all-start.1 = ((f32[32,1,2816]{2,1,0:T(1,128)}), f32[32,1,2816]{2,1,0:T(1,128)S(1)}, u32[]{:S(2)}, u32[]{:S(2)}) async-start(f32[32,1,2816]{2,1,0:T(1,128)} %reshape.1231), calls=%async_computation.1 | async-start | bytes 720896 | tf_op jit(solution)/shard_map/all_to_all | solution.py:199
  99.9 17.5 %all-to-all-start.2 = ((f32[32,1,2816]{2,1,0:T(1,128)}), f32[32,1,2816]{2,1,0:T(1,128)S(1)}, u32[]{:S(2)}, u32[]{:S(2)}) async-start(f32[32,1,2816]{2,1,0:T(1,128)} %reshape.1233), calls=%async_computation.2 | async-start | bytes 720896 | tf_op jit(solution)/shard_map/all_to_all | solution.py:202
  199.8 34.5 %all-to-all-start.3 = ((f32[32,1,9856]{2,1,0:T(1,128)}), f32[32,1,9856]{2,1,0:T(1,128)}, u32[]{:S(2)}, u32[]{:S(2)}) async-start(f32[32,1,9856]{2,1,0:T(1,128)} %reshape.1235), calls=%async_computation.3 | async-start | bytes 2523136 | tf_op jit(solution)/shard_map/all_to_all | solution.py:214
  234.3 34.2 %all-to-all-start.4 = ((f32[32,1,9856]{2,1,0:T(1,128)}), f32[32,1,9856]{2,1,0:T(1,128)}, u32[]{:S(2)}, u32[]{:S(2)}) async-start(f32[32,1,9856]{2,1,0:T(1,128)} %reshape.1237), calls=%async_computation.4 | async-start | bytes 2523136 | tf_op jit(solution)/shard_map/all_to_all | solution.py:215
  238.2 101.7 %copy-start.47 = (f32[32,64]{0,1:T(8,128)}, f32[32,64]{0,1:T(8,128)S(1)}, u32[]{:S(2)}) copy-start(f32[32,64]{0,1:T(8,128)S(1)} %copy.677) | copy-start | bytes 24580
  362.2 12.5 %copy-start.4 = (f32[7,32,64,64]{3,1,2,0:T(8,128)S(1)}, f32[7,32,64,64]{3,1,2,0:T(8,128)}, u32[]{:S(2)}) copy-start(f32[7,32,64,64]{3,1,2,0:T(8,128)} %get-tuple-element.32) | copy-start | bytes 11010052
  532.0 20.1 %copy-start.19 = (f32[1,4,64,512]{3,2,1,0:T(8,128)}, f32[1,4,64,512]{3,2,1,0:T(8,128)S(1)}, u32[]{:S(2)}) copy-start(f32[1,4,64,512]{3,2,1,0:T(8,128)S(1)} %get-tuple-element.55) | copy-start | bytes 1572868
  533.4 18.3 %all-to-all-start.6 = ((f32[1,256,512]{2,0,1:T(1,128)}), f32[1,256,512]{2,0,1:T(1,128)S(1)}, u32[]{:S(2)}, u32[]{:S(2)}) async-start(f32[1,256,512]{2,0,1:T(1,128)} %copy.684), calls=%async_computation.6 | async-start | bytes 1048576 | tf_op jit(solution)/shard_map/all_to_all | solution.py:196
  567.1 16.2 %all-to-all-start.7 = ((f32[32,1,1408]{2,1,0:T(1,128)}), f32[32,1,1408]{2,1,0:T(1,128)S(1)}, u32[]{:S(2)}, u32[]{:S(2)}) async-start(f32[32,1,1408]{2,1,0:T(1,128)} %reshape.1241), calls=%async_computation.7 | async-start | bytes 360448 | tf_op jit(solution)/shard_map/all_to_all | solution.py:199
  583.3 14.1 %all-to-all-start.8 = ((f32[32,1,1408]{2,1,0:T(1,128)}), f32[32,1,1408]{2,1,0:T(1,128)S(1)}, u32[]{:S(2)}, u32[]{:S(2)}) async-start(f32[32,1,1408]{2,1,0:T(1,128)} %reshape.1243), calls=%async_computation.8 | async-start | bytes 360448 | tf_op jit(solution)/shard_map/all_to_all | solution.py:202
  618.6 15.2 %all-to-all-start.10 = ((f32[32,1,2816]{2,1,0:T(1,128)}), f32[32,1,2816]{2,1,0:T(1,128)S(1)}, u32[]{:S(2)}, u32[]{:S(2)}) async-start(f32[32,1,2816]{2,1,0:T(1,128)} %reshape.1245), calls=%async_computation.10 | async-start | bytes 720896 | tf_op jit(solution)/shard_map/all_to_all | solution.py:215
  633.8 17.8 %all-to-all-start.9 = ((f32[32,1,2816]{2,1,0:T(1,128)}), f32[32,1,2816]{2,1,0:T(1,128)S(1)}, u32[]{:S(2)}, u32[]{:S(2)}) async-start(f32[32,1,2816]{2,1,0:T(1,128)} %reshape.1247), calls=%async_computation.9 | async-start | bytes 720896 | tf_op jit(solution)/shard_map/all_to_all | solution.py:214
  776.8 16.9 %all-to-all-start.13 = ((f32[32,1,1408]{2,1,0:T(1,128)}), f32[32,1,1408]{2,1,0:T(1,128)S(1)}, u32[]{:S(2)}, u32[]{:S(2)}) async-start(f32[32,1,1408]{2,1,0:T(1,128)} %reshape.1251), calls=%async_computation.13 | async-start | bytes 360448 | tf_op jit(solution)/shard_map/all_to_all | solution.py:199
  793.7 14.5 %all-to-all-start.14 = ((f32[32,1,1408]{2,1,0:T(1,128)}), f32[32,1,1408]{2,1,0:T(1,128)S(1)}, u32[]{:S(2)}, u32[]{:S(2)}) async-start(f32[32,1,1408]{2,1,0:T(1,128)} %reshape.1253), calls=%async_computation.14 | async-start | bytes 360448 | tf_op jit(solution)/shard_map/all_to_all | solution.py:202
  834.7 18.4 %all-to-all-start.15 = ((f32[32,1,1408]{2,1,0:T(1,128)}), f32[32,1,1408]{2,1,0:T(1,128)S(1)}, u32[]{:S(2)}, u32[]{:S(2)}) async-start(f32[32,1,1408]{2,1,0:T(1,128)} %reshape.1255), calls=%async_computation.15 | async-start | bytes 360448 | tf_op jit(solution)/shard_map/all_to_all | solution.py:214
  853.1 14.3 %all-to-all-start.16 = ((f32[32,1,1408]{2,1,0:T(1,128)}), f32[32,1,1408]{2,1,0:T(1,128)S(1)}, u32[]{:S(2)}, u32[]{:S(2)}) async-start(f32[32,1,1408]{2,1,0:T(1,128)} %reshape.1257), calls=%async_computation.16 | async-start | bytes 360448 | tf_op jit(solution)/shard_map/all_to_all | solution.py:215
  902.3 110.5 %all-to-all-start.17 = ((f32[4,1,32768]{2,1,0:T(1,128)}), f32[4,1,32768]{2,1,0:T(1,128)S(1)}, u32[]{:S(2)}, u32[]{:S(2)}) async-start(f32[4,1,32768]{2,1,0:T(1,128)} %reshape.1259), calls=%async_computation.17 | async-start | bytes 1048576 | tf_op jit(solution)/shard_map/all_to_all | solution.py:219
  949.7 13.3 %copy-start.24 = (f32[1,4,64,512]{3,2,1,0:T(8,128)S(1)}, f32[1,4,64,512]{3,2,1,0:T(8,128)}, u32[]{:S(2)}) copy-start(f32[1,4,64,512]{3,2,1,0:T(8,128)} %get-tuple-element.51) | copy-start | bytes 1572868
  997.8 14.0 %copy-start.26 = (f32[1,4,64,512]{3,1,2,0:T(4,128)S(1)}, f32[1,4,64,512]{3,1,2,0:T(4,128)}, u32[]{:S(2)}) copy-start(f32[1,4,64,512]{3,1,2,0:T(4,128)} %get-tuple-element.66) | copy-start | bytes 1572868
  1075.7 2.7 collective-permute-start
  1077.3 4.4 collective-permute-start.1
  1092.7 9.1 collective-permute-start.2
  1099.3 5.7 collective-permute-start.3
  1112.5 12.8 %copy-start.8 = (f32[15,128,256]{2,1,0:T(8,128)S(1)}, f32[15,128,256]{2,1,0:T(8,128)}, u32[]{:S(2)}) copy-start(f32[15,128,256]{2,1,0:T(8,128)} %get-tuple-element.41) | copy-start | bytes 5898244
  1112.5 12.8 %copy-start.9 = (f32[15,128,256]{2,1,0:T(8,128)S(1)}, f32[15,128,256]{2,1,0:T(8,128)}, u32[]{:S(2)}) copy-start(f32[15,128,256]{2,1,0:T(8,128)} %get-tuple-element.42) | copy-start | bytes 5898244
  1112.5 12.8 %copy-start.34 = (f32[1,128,256]{2,1,0:T(8,128)S(1)}, f32[1,128,256]{2,1,0:T(8,128)}, u32[]{:S(2)}) copy-start(f32[1,128,256]{2,1,0:T(8,128)} %get-tuple-element.76) | copy-start | bytes 393220
  1112.5 12.8 %copy-start.35 = (f32[128,256]{1,0:T(8,128)S(1)}, f32[128,256]{1,0:T(8,128)}, u32[]{:S(2)}) copy-start(f32[128,256]{1,0:T(8,128)} %get-tuple-element.77) | copy-start | bytes 393220
  1112.5 12.8 %copy-start.38 = (f32[1,128,256]{2,1,0:T(8,128)S(1)}, f32[1,128,256]{2,1,0:T(8,128)}, u32[]{:S(2)}) copy-start(f32[1,128,256]{2,1,0:T(8,128)} %get-tuple-element.46) | copy-start | bytes 393220
  1125.3 11.1 copy-start.10
  1125.3 11.0 copy-start.46
  (41 other events, 158.9 us)
where the time goes:
time: 1160 us; the launch traced here: 1150 us
  local copies, waits for them, and re-layouts  392 us (34%)
  matrix products  270 us (23%)
  other arithmetic  200 us (17%)
  blocking collectives  132 us (11%)
  waiting for transfers between devices  80.7 us (7%)
  starting transfers between devices  77.5 us (7%)
    dot_general x84, matrix products, product(): return jnp.einsum(form, left, right, precision=lax.Precision.HIGHEST)  270 us
    all_to_all x2, blocking collectives, inverse(): lax.all_to_all(pencil, 'col', split_axis=2, concat_axis=1, tiled=True)  116 us
    unnamed x150, local copies, waits for them, and re-layouts  111 us
    another operation x2, local copies, waits for them, and re-layouts, coarsen(): return source.reshape(rows_out, COARSE, cols_out, COARSE).mean(axis=(1, 3))  69.7 us
    another operation x4, other arithmetic, flow_update(): return jnp.stack([next_u, next_v, next_w])  41.6 us
    reduce_sum x3, other arithmetic, coarsen(): return source.reshape(rows_out, COARSE, cols_out, COARSE).mean(axis=(1, 3))  39.8 us
    all_to_all x2, waiting for transfers between devices, forward(): lax.all_to_all(stacked, 'col', split_axis=1, concat_axis=2, tiled=True)  39.6 us
    unnamed x8, other arithmetic  37.8 us
  transfers between devices with their start and end apart: 19, of which 12 were waited for; matrix products, arithmetic and copies ran while one was open for 22% of the time, Pallas kernels for 0%

commit v1 on v0

v1 whole, which is shorter than its diff:
```python
import functools
import math

import jax
import jax.numpy as jnp
from jax import lax
from jax.experimental import pallas as pl
from jax.experimental.pallas import tpu as pltpu
from jax.sharding import PartitionSpec as P

COARSE = 2
GRAVITY = 1.0
SURFACE_STEP = 0.05
FLOW_STEP = 0.5
VISCOSITY = 0.2
DECAY_RATE = 0.05

F32 = jnp.float32
BF16 = jnp.bfloat16
VMEM_LIMIT = 60 * 1024 * 1024


def round_up(value, step):
    return -(-value // step) * step


class Plan:
    def __init__(self, rows, cols, tile):
        self.R, self.C = rows, cols
        self.NYL, self.NXL = tile
        self.NY, self.NX = rows * self.NYL, cols * self.NXL
        self.XC = self.NXL // rows
        self.Q = max(1, 128 // self.XC)
        self.NYF = self.NYL // self.Q
        self.W = self.Q * self.XC
        self.KEPT_Y = self.NY // 3 + 1
        self.KEPT_X = self.NX // 3 + 1
        self.M = round_up(-(-(-(-self.KEPT_Y // rows)) // cols), 8)
        self.KY = cols * self.M
        self.J = round_up(-(-self.KEPT_X // cols), 128)
        self.L2 = 2 * self.XC
        self.PEERS = rows * cols
        self.NYC, self.NXC = self.NYF // COARSE, self.W // COARSE


def split(x):
    hi = x.astype(BF16)
    return hi, (x - hi.astype(F32)).astype(BF16)


def dot(a, b):
    return jnp.dot(a, b, preferred_element_type=F32)


def dot3(a, b):
    return dot(a[0], b[0]) + (dot(a[0], b[1]) + dot(a[1], b[0]))


def cat(parts, axis):
    return parts[0] if len(parts) == 1 else jnp.concatenate(parts, axis=axis)


def turn(numer, denom):
    numer %= denom
    exact = {0: (1.0, 0.0), 1: (0.0, 1.0), 2: (-1.0, 0.0), 3: (0.0, -1.0)}
    if 4 * numer % denom == 0:
        return exact[4 * numer // denom]
    angle = 2.0 * math.pi * numer / denom
    return math.cos(angle), math.sin(angle)


def combine(terms):
    total = None
    for factor, value in terms:
        if factor == 0.0:
            continue
        if total is None:
            total = value if factor == 1.0 else (-value if factor == -1.0 else factor * value)
        elif factor == 1.0:
            total = total + value
        elif factor == -1.0:
            total = total - value
        else:
            total = total + factor * value
    return total


def mirrored(index, count):
    if index == 0 or 2 * index == count:
        return ((index, 1.0),)
    return ((index, 1.0), (count - index, -1.0))


def unfold(x, plan):
    return cat([x[:, h * plan.XC : (h + 1) * plan.XC] for h in range(plan.Q)], 0)


def fold(x, plan):
    return cat([x[h * plan.NYF : (h + 1) * plan.NYF] for h in range(plan.Q)], 1)


def swap_halves(x, half):
    if 2 * half == 128:
        return pltpu.roll(x, half, 1)
    return jnp.concatenate([x[:, half:], x[:, :half]], axis=1)


def y_forward(plan, blocks, field, tab, out_ref):
    for k0 in range(plan.R // 2 + 1):
        even = combine([(turn(k0 * r, plan.R)[0], blocks[r]) for r in range(plan.R)])
        odd = combine([(turn(k0 * r, plan.R)[1], blocks[r]) for r in range(plan.R)])
        even = split(unfold(even, plan))
        if odd is None:
            odd = tuple(jnp.zeros_like(e) for e in even)
        else:
            odd = split(unfold(odd, plan))
        for k, sign in mirrored(k0, plan.R):
            if sign > 0:
                pos, neg = odd, [-o for o in odd]
            else:
                pos, neg = [-o for o in odd], odd
            rhs = [
                jnp.concatenate(
                    [
                        jnp.concatenate([even[i], pos[i]], axis=1),
                        jnp.concatenate([neg[i], even[i]], axis=1),
                    ],
                    axis=0,
                )
                for i in range(2)
            ]
            lines = dot3((tab[0][k], tab[1][k]), rhs)
            for c in range(plan.C):
                out_ref[k * plan.C + c, field * plan.M : (field + 1) * plan.M, :] = lines[
                    c * plan.M : (c + 1) * plan.M
                ]


def y_inverse(plan, buf_ref, fields, tab, work_ref):
    L2, M, C = plan.L2, plan.M, plan.C
    lane = lax.broadcasted_iota(jnp.int32, (1, L2), 1)
    flip = jnp.where(lane < plan.XC, 1.0, -1.0).astype(F32)
    for k0 in range(plan.R // 2 + 1):
        total = None
        for k, sign in mirrored(k0, plan.R):
            tops, bottoms = [], []
            for f in range(fields):
                lines = cat(
                    [buf_ref[k * C + c, f * M : (f + 1) * M, :] for c in range(C)], 0
                )
                tops.append(lines)
                bottoms.append(swap_halves(lines, plan.XC) * flip)
            rhs = split(jnp.concatenate([cat(tops, 1), cat(bottoms, 1)], axis=0))
            part = dot3((tab[0][k], tab[1][k]), rhs)
            if sign > 0:
                total = part
            else:
                total = total + part * cat([flip] * fields, 1)
        work_ref[k0] = total


def y_block(plan, work_ref, field, r):
    L2 = plan.L2
    lane = lax.broadcasted_iota(jnp.int32, (1, L2), 1)
    total = None
    for k0 in range(plan.R // 2 + 1):
        c, s = turn(k0 * r, plan.R)
        factor = jnp.where(lane < plan.XC, c, s).astype(F32)
        part = work_ref[k0, :, field * L2 : (field + 1) * L2] * factor
        total = part if total is None else total + part
    if L2 == 128 and plan.Q == 2:
        both = total + pltpu.roll(total, plan.XC, 1)
        return jnp.where(lane < plan.XC, both[: plan.NYF], both[plan.NYF :])
    return fold(total[:, : plan.XC] + total[:, plan.XC :], plan)


def pack_kernel(plan, potential_ref, height_ref, out_ref):
    for r in range(plan.R):
        for f, ref in enumerate((potential_ref, height_ref)):
            out_ref[r, f * plan.NYF : (f + 1) * plan.NYF, :] = fold(
                ref[:, r * plan.XC : (r + 1) * plan.XC], plan
            )


def first_kernel(plan, in_ref, hi_ref, lo_ref, out_ref, height_ref):
    for f in range(2):
        blocks = [in_ref[r, f * plan.NYF : (f + 1) * plan.NYF, :] for r in range(plan.R)]
        y_forward(plan, blocks, f, (hi_ref, lo_ref), out_ref)
    for r in range(plan.R):
        height_ref[r] = in_ref[r, plan.NYF :, :]


def x_kernel(plan, fields, wanted, place_ref, in_ref, fh, fl, ih, il, out_ref, u_ref):
    R, C, M, J, XC, NXL = plan.R, plan.C, plan.M, plan.J, plan.XC, plan.NXL
    rows, outs = fields * M, len(wanted)
    lines = []
    for c in range(C):
        halves = []
        for h in range(2):
            halves.append(
                cat([in_ref[r * C + c, :, h * XC : (h + 1) * XC] for r in range(R)], 1)
            )
        lines.append(jnp.concatenate(halves, axis=0))
    row_k0, row_k1 = place_ref[0], place_ref[1]
    ky_index = R * (row_k1 + lax.broadcasted_iota(jnp.int32, (M, J), 0)) + row_k0
    ky = ky_index.astype(F32) * (2.0 * math.pi / plan.NY)
    y_weight = jnp.where(
        ky_index == 0, 1.0, jnp.where(ky_index < plan.KEPT_Y, 2.0, 0.0)
    ).astype(F32)
    slot = 0
    slots = []
    for j0 in range(C // 2 + 1):
        even = split(combine([(turn(j0 * c, C)[0], lines[c]) for c in range(C)]))
        odd = combine([(turn(j0 * c, C)[1], lines[c]) for c in range(C)])
        odd = None if odd is None else split(odd)
        u_sum = v_sum = None
        for j, sign in mirrored(j0, C):
            table = (fh[j], fl[j])
            of_even = dot3(even, table)
            p_all, q_all = of_even[:, :J], of_even[:, J:]
            if odd is not None:
                of_odd = dot3(odd, table)
                p_all = p_all - sign * of_odd[:, J:]
                q_all = q_all + sign * of_odd[:, :J]
            kx_index = C * lax.broadcasted_iota(jnp.int32, (M, J), 1) + j
            kx = kx_index.astype(F32) * (2.0 * math.pi / plan.NX)
            x_weight = jnp.where(
                kx_index == 0, 1.0, jnp.where(kx_index < plan.KEPT_X, 2.0, 0.0)
            ).astype(F32)
            weight = x_weight * y_weight * (1.0 / (plan.NX * plan.NY))
            size = jnp.sqrt(kx * kx + ky * ky)
            coef = []
            for f in range(fields):
                top, low = slice(f * M, (f + 1) * M), slice(rows + f * M, rows + (f + 1) * M)
                coef.append(
                    (
                        p_all[top] * weight,
                        q_all[top] * weight,
                        p_all[low] * weight,
                        q_all[low] * weight,
                    )
                )
            tops, lows = [], []
            for f, kind in wanted:
                cc, cs, sc, ss = coef[f]
                if kind == "dx":
                    new = (kx * cs, -kx * cc, kx * ss, -kx * sc)
                elif kind == "dy":
                    new = (ky * sc, ky * ss, -ky * cc, -ky * cs)
                else:
                    factor = size
                    for _ in range(kind - 1):
                        factor = factor * size
                    new = (factor * cc, factor * cs, factor * sc, factor * ss)
                tops.append((new[0], new[1]))
                lows.append((new[2], new[3]))
            p_new = cat([t[0] for t in tops] + [t[0] for t in lows], 0)
            q_new = cat([t[1] for t in tops] + [t[1] for t in lows], 0)
            p_new, q_new = split(p_new), split(q_new)
            back = (ih[j], il[j])
            u = dot3([jnp.concatenate([p_new[i], q_new[i]], axis=1) for i in range(2)], back)
            u_sum = u if u_sum is None else u_sum + u
            if odd is not None:
                v = dot3(
                    [jnp.concatenate([q_new[i], -p_new[i]], axis=1) for i in range(2)], back
                )
                v_sum = v if v_sum is None else v_sum - v
        u_ref[slot] = u_sum
        slots.append((j0, slot, None if v_sum is None else slot + 1))
        if v_sum is not None:
            u_ref[slot + 1] = v_sum
        slot += 1 if v_sum is None else 2
    half = outs * M
    for c in range(C):
        terms = []
        for j0, u_slot, v_slot in slots:
            cs, sn = turn(j0 * c, C)
            terms.append((cs, u_slot))
            if v_slot is not None:
                terms.append((sn, v_slot))
        for r in range(0, R):
            lanes = slice(r * XC, (r + 1) * XC)
            top = combine([(a, u_ref[s, :half, lanes]) for a, s in terms if a != 0.0])
            low = combine([(a, u_ref[s, half:, lanes]) for a, s in terms if a != 0.0])
            out_ref[r * C + c] = jnp.concatenate([top, low], axis=1)


def second_kernel(
    plan, buf_ref, height_ref, ih, il, fh, fl,
    out_ref, vertical_ref, third_ref, slope_ref, rate_ref, energy_ref, coarse_ref, work_ref,
):
    y_inverse(plan, buf_ref, 7, (ih, il), work_ref)
    pool_y, pool_x = pools(plan.NYC, plan.NYF, plan.W, plan.NXC)
    blocks = []
    for r in range(plan.R):
        height = height_ref[r]
        vert, curve, cube, pot_dx, pot_dy, height_dx, height_dy = [
            y_block(plan, work_ref, f, r) for f in range(7)
        ]
        square = 0.5 * height * height
        vertical_ref[r] = vert + height * curve + square * cube
        third_ref[r] = -square * curve
        slope_ref[r] = height_dx * height_dx + height_dy * height_dy
        rate_ref[r] = -(height_dx * pot_dx + height_dy * pot_dy)
        energy_ref[r] = -GRAVITY * height - 0.5 * (pot_dx * pot_dx + pot_dy * pot_dy)
        coarse_ref[r] = jnp.concatenate(
            [pooled(pot_dx, pool_y, pool_x), pooled(pot_dy, pool_y, pool_x)], axis=1
        )
        blocks.append(-height * vert)
    y_forward(plan, blocks, 0, (fh, fl), out_ref)


def third_kernel(
    plan, buf_ref, height_ref, vertical_in, third_in, ih, il, fh, fl, out_ref, vertical_ref, work_ref
):
    y_inverse(plan, buf_ref, 2, (ih, il), work_ref)
    blocks = []
    for r in range(plan.R):
        height = height_ref[r]
        vert, curve = [y_block(plan, work_ref, f, r) for f in range(2)]
        vertical_ref[r] = vertical_in[r] + vert + height * curve
        blocks.append(third_in[r] - height * vert)
    y_forward(plan, blocks, 0, (fh, fl), out_ref)


def rates_kernel(
    plan, buf_ref, vertical_in, slope_ref, rate_ref, energy_ref, coarse_ref, ih, il, out_ref, work_ref
):
    y_inverse(plan, buf_ref, 1, (ih, il), work_ref)
    N = plan.NYF
    for r in range(plan.R):
        vertical = vertical_in[r] + y_block(plan, work_ref, 0, r)
        lift = (1.0 + slope_ref[r]) * vertical
        out_ref[r, :N, :] = rate_ref[r] + lift
        out_ref[r, N : 2 * N, :] = energy_ref[r] + 0.5 * lift * vertical
        out_ref[r, 2 * N :, :] = coarse_ref[r]


def pools(rows_out, rows_in, cols_in, cols_out):
    def pool(shape, out_dim):
        i = lax.broadcasted_iota(jnp.int32, shape, out_dim)
        k = lax.broadcasted_iota(jnp.int32, shape, 1 - out_dim)
        return jnp.where((k >= COARSE * i) & (k < COARSE * (i + 1)), 1.0 / COARSE, 0.0).astype(BF16)

    return pool((rows_out, rows_in), 0), pool((cols_in, cols_out), 1)


def pooled(x, pool_y, pool_x):
    hi, lo = split(x)
    low = (x - hi.astype(F32) - lo.astype(F32)).astype(BF16)
    lines = dot(hi, pool_x) + (dot(lo, pool_x) + dot(low, pool_x))
    hi, lo = split(lines)
    low = (lines - hi.astype(F32) - lo.astype(F32)).astype(BF16)
    return dot(pool_y, hi) + (dot(pool_y, lo) + dot(pool_y, low))


def tile_kernel(
    plan, in_ref, height_ref, rate_ref, energy_ref, pressure_ref, u_ref, v_ref, column_ref
):
    R, Q, XC, N = plan.R, plan.Q, plan.XC, plan.NYF
    for f, ref in enumerate((rate_ref, energy_ref)):
        for h in range(Q):
            ref[h * N : (h + 1) * N, :] = cat(
                [in_ref[r, f * N : (f + 1) * N, h * XC : (h + 1) * XC] for r in range(R)], 1
            )
    NC, XH = plan.NYC, XC // COARSE
    for f, ref in enumerate((u_ref, v_ref)):
        for h in range(Q):
            base = f * plan.NXC + h * XH
            ref[h * NC : (h + 1) * NC, :] = cat(
                [in_ref[r, 2 * N :, base : base + XH] for r in range(R)], 1
            )
    pool_y, pool_x = pools(plan.NYL // COARSE, plan.NYL, plan.NXL, plan.NXL // COARSE)
    pressure = GRAVITY * pooled(height_ref[...] + SURFACE_STEP * rate_ref[...], pool_y, pool_x)
    pressure_ref[...] = pressure
    first = jnp.transpose(pressure[:, :128])
    last = jnp.transpose(pressure[:, -128:])
    column_ref[0:8, :] = first[0:8]
    column_ref[8:16, :] = last[-8:]


def flow_kernel(
    levels, decay_ref, prev_ref, cur_ref, next_ref, rows_ref, cols_ref,
    pressure_ref, prow_ref, pcol_ref, u_ref, v_ref, out_ref,
):
    level = pl.program_id(0)
    ny, nx = cur_ref.shape[2:]
    lane = lax.broadcasted_iota(jnp.int32, (ny, nx), 1)
    line = lax.broadcasted_iota(jnp.int32, (ny, nx), 0)

    def around(x, south, north, west, east):
        return (
            jnp.where(lane == nx - 1, east, pltpu.roll(x, nx - 1, 1)),
            jnp.where(lane == 0, west, pltpu.roll(x, 1, 1)),
            jnp.where(line == ny - 1, north, pltpu.roll(x, ny - 1, 0)),
            jnp.where(line == 0, south, pltpu.roll(x, 1, 0)),
        )

    cols = jnp.transpose(cols_ref[0])
    top_u, top_v = u_ref[...], v_ref[...]
    is_top = level == 0

    def derivs(q, top):
        mid = cur_ref[q, 0]
        east, west, north, south = around(
            mid,
            rows_ref[0, q : q + 1, :],
            rows_ref[0, 3 + q : 4 + q, :],
            cols[:, q : q + 1],
            cols[:, 3 + q : 4 + q],
        )
        above = jnp.where(is_top, top, prev_ref[q, 0])
        below = next_ref[q, 0]
        lap = (east + west) + (north + south) + (above + below) - 6.0 * mid
        return mid, 0.5 * (east - west), 0.5 * (north - south), 0.5 * (above - below), lap

    u, u_dx, u_dy, u_dz, u_lap = derivs(0, top_u)
    v, v_dx, v_dy, v_dz, v_lap = derivs(1, top_v)
    w, w_dx, w_dy, w_dz, w_lap = derivs(2, jnp.zeros_like(top_u))
    drift_u = top_u * decay_ref[level, 0]
    drift_v = top_v * decay_ref[level, 0]
    vort_x = w_dy - v_dz
    vort_y = u_dz - w_dx
    vort_z = v_dx - u_dy
    pcols = jnp.transpose(pcol_ref[...])
    p_east, p_west, p_north, p_south = around(
        pressure_ref[...], prow_ref[0:1, :], prow_ref[1:2, :], pcols[:, 0:1], pcols[:, 1:2]
    )
    load = 0.5 * decay_ref[level, 1]
    load_x = load * (p_east - p_west)
    load_y = load * (p_north - p_south)

    def advance(mid, dx, dy, dz, lap, force):
        return mid + FLOW_STEP * (VISCOSITY * lap + force - (u * dx + v * dy + w * dz))

    out_ref[0, 0] = advance(u, u_dx, u_dy, u_dz, u_lap, drift_v * vort_z - load_x)
    out_ref[1, 0] = advance(v, v_dx, v_dy, v_dz, v_lap, -drift_u * vort_z - load_y)
    out_ref[2, 0] = advance(w, w_dx, w_dy, w_dz, w_lap, drift_u * vort_y - drift_v * vort_x)


def parts(table):
    hi = lax.reduce_precision(table, 8, 7)
    return hi.astype(BF16), (table - hi).astype(BF16)


def angles(numbers, places, total):
    numbers, places = lax.optimization_barrier((numbers, places))
    return (numbers * places % total).astype(F32) * (2.0 * math.pi / total)


def make_tables(plan):
    k0 = jnp.arange(plan.R, dtype=jnp.int32)[:, None, None]
    k1 = jnp.arange(plan.KY, dtype=jnp.int32)
    y = jnp.arange(plan.NYL, dtype=jnp.int32)
    angle = angles(plan.R * k1[None, :, None] + k0, y[None, None, :], plan.NY)
    y_fwd = parts(jnp.concatenate([jnp.cos(angle), jnp.sin(angle)], axis=2))
    angle = angles(plan.R * k1[None, None, :] + k0, y[None, :, None], plan.NY)
    y_inv = parts(jnp.concatenate([jnp.cos(angle), jnp.sin(angle)], axis=2))
    j0 = jnp.arange(plan.C, dtype=jnp.int32)[:, None, None]
    j1 = jnp.arange(plan.J, dtype=jnp.int32)
    x = jnp.arange(plan.NXL, dtype=jnp.int32)
    angle = angles(plan.C * j1[None, None, :] + j0, x[None, :, None], plan.NX)
    x_fwd = parts(jnp.concatenate([jnp.cos(angle), jnp.sin(angle)], axis=2))
    angle = angles(plan.C * j1[None, :, None] + j0, x[None, None, :], plan.NX)
    x_inv = parts(jnp.concatenate([jnp.cos(angle), jnp.sin(angle)], axis=1))
    return y_fwd, y_inv, x_fwd, x_inv


def call(kernel, name, outs, scratch=(), smem=0):
    vmem = pl.BlockSpec(memory_space=pltpu.VMEM)

    def run(*args):
        specs = [pl.BlockSpec(memory_space=pltpu.SMEM)] * smem + [vmem] * (len(args) - smem)
        shapes = [jax.ShapeDtypeStruct(s, F32) for s in outs]
        return pl.pallas_call(
            kernel,
            out_shape=shapes,
            in_specs=specs,
            out_specs=[vmem] * len(outs),
            scratch_shapes=[pltpu.VMEM(s, F32) for s in scratch],
            compiler_params=pltpu.CompilerParams(vmem_limit_bytes=VMEM_LIMIT),
            name=name,
        )(*args)

    return run


def exchange(x, axes):
    return lax.all_to_all(x, axes, split_axis=0, concat_axis=0, tiled=True)


def shift(x, axis, step):
    peers = lax.axis_size(axis)
    return lax.ppermute(x, axis, [(i, (i + step) % peers) for i in range(peers)])


def local(surface_height, surface_potential, velocity):
    plan = Plan(lax.axis_size("row"), lax.axis_size("col"), surface_height.shape)
    R, M, W, N, L2 = plan.R, plan.M, plan.W, plan.NYF, plan.L2
    bind = lambda kernel, *rest: functools.partial(kernel, plan, *rest)
    both = ("row", "col")
    pencil = (R, N, W)
    work = lambda f: (R // 2 + 1, plan.NYL, f * L2)
    spec = lambda f: (plan.PEERS, f * M, L2)

    (packed,) = call(bind(pack_kernel), "pack", [(R, 2 * N, W)])(surface_potential, surface_height)
    packed = exchange(packed, "row")

    levels, ny, nx = velocity.shape[1:]
    rows = jnp.concatenate(
        [shift(velocity[:, :, -1, :], "row", 1), shift(velocity[:, :, 0, :], "row", -1)], axis=0
    )
    cols = jnp.concatenate(
        [shift(velocity[:, :, :, -1], "col", 1), shift(velocity[:, :, :, 0], "col", -1)], axis=0
    )
    pad = lambda e: jnp.pad(jnp.swapaxes(e, 0, 1), ((0, 0), (0, 2), (0, 0)))
    rows, cols = pad(rows), pad(cols)
    mid = jnp.arange(levels, dtype=F32) + 0.5
    decay = jnp.stack([jnp.exp(-2.0 * DECAY_RATE * mid), jnp.exp(-DECAY_RATE * mid)], axis=1)

    y_fwd, y_inv, x_fwd, x_inv = make_tables(plan)
    place = jnp.stack([lax.axis_index("row"), lax.axis_index("col") * M]).astype(jnp.int32)

    def x_stage(buf, fields, wanted):
        outs = len(wanted)
        slots = 2 * (plan.C // 2 + 1) - (1 if plan.C == 1 else 2)
        kernel = bind(x_kernel, fields, wanted)
        (out,) = call(
            kernel, "x%d" % outs, [spec(outs)], [(slots, 2 * outs * M, plan.NXL)], smem=1
        )(place, buf, *x_fwd, *x_inv)
        return exchange(out, both)

    first, height = call(bind(first_kernel), "y0", [spec(2), pencil])(packed, *y_fwd)
    first = x_stage(
        exchange(first, both),
        2,
        ((0, 1), (0, 2), (0, 3), (0, "dx"), (0, "dy"), (1, "dx"), (1, "dy")),
    )
    second, vertical, third, slope, rate, energy, coarse = call(
        bind(second_kernel),
        "y1",
        [spec(1)] + [pencil] * 5 + [(R, plan.NYC, 2 * plan.NXC)],
        [work(7)],
    )(first, height, *y_inv, *y_fwd)
    second = x_stage(exchange(second, both), 1, ((0, 1), (0, 2)))
    last, vertical = call(bind(third_kernel), "y2", [spec(1), pencil], [work(2)])(
        second, height, vertical, third, *y_inv, *y_fwd
    )
    last = x_stage(exchange(last, both), 1, ((0, 1),))
    (rates,) = call(bind(rates_kernel), "y3", [(R, 2 * N + plan.NYC, W)], [work(1)])(
        last, vertical, slope, rate, energy, coarse, *y_inv
    )
    rates = exchange(rates, "row")
    tile = surface_height.shape
    height_rate, potential_rate, pressure, surface_u, surface_v, column = call(
        bind(tile_kernel), "tile", [tile, tile] + [(ny, nx)] * 3 + [(16, ny)]
    )(rates, surface_height)

    prow = jnp.concatenate(
        [shift(pressure[-1:], "row", 1), shift(pressure[:1], "row", -1)], axis=0
    )
    pcol = jnp.concatenate(
        [shift(column[-1:], "col", 1), shift(column[:1], "col", -1)], axis=0
    )
    prow, pcol = [jnp.pad(e, ((0, 6), (0, 0))) for e in (prow, pcol)]

    block = (3, 1, ny, nx)
    at = lambda step: pl.BlockSpec(
        block, lambda l: (0, jnp.clip(l + step, 0, levels - 1), 0, 0)
    )
    whole = lambda x: pl.BlockSpec(x.shape, lambda l: (0,) * x.ndim)
    per_level = lambda x: pl.BlockSpec((1,) + x.shape[1:], lambda l: (l, 0, 0))
    velocity_next = pl.pallas_call(
        functools.partial(flow_kernel, levels),
        grid=(levels,),
        out_shape=jax.ShapeDtypeStruct(velocity.shape, F32),
        in_specs=[pl.BlockSpec(memory_space=pltpu.SMEM), at(-1), at(0), at(1)]
        + [per_level(rows), per_level(cols)]
        + [whole(x) for x in (pressure, prow, pcol, surface_u, surface_v)],
        out_specs=at(0),
        compiler_params=pltpu.CompilerParams(vmem_limit_bytes=VMEM_LIMIT),
        name="flow",
    )(decay, velocity, velocity, velocity, rows, cols, pressure, prow, pcol, surface_u, surface_v)
    return height_rate, potential_rate, velocity_next


def solution(mesh):
    placed = (P("row", "col"), P("row", "col"), P(None, None, "row", "col"))
    return jax.shard_map(
        local,
        mesh=mesh,
        in_specs=placed,
        out_specs=placed,
        check_vma=False,
    )
```

time: 1160 us -> 312 us (0.27)
  local copies, waits for them, and re-layouts: 392 us -> 17.7 us
  matrix products: 270 us -> 0 us
  other arithmetic: 200 us -> 33.2 us
  Pallas kernels: 0 us -> 81.4 us
  blocking collectives: 132 us -> 71.2 us
  starting transfers between devices: 77.5 us -> 29.8 us
    dot_general x84 -> x0, matrix products: 270 us -> none  [product(): return jnp.einsum(form, left, right, precision=lax.Precision.HIGHEST)]
    unnamed x150 -> x10, local copies, waits for them, and re-layouts: 111 us -> 7.6 us
    another operation x22 -> x1, local copies, waits for them, and re-layouts: 82.6 us -> 0.69 us  [local(): jnp.stack([jnp.exp(-2.0 * DECAY_RATE * mid), jnp.exp(-DECAY_RATE * mid)],...]
    pallas_call x0 -> x10, Pallas kernels: none -> 81.4 us  [the longest x9 62.1 us: run(): pl.pallas_call(kernel, out_shape=shapes, in_specs=specs, out_specs=[vmem]...]
    reshape x14 -> x0, local copies, waits for them, and re-layouts: 70.2 us -> none  [the longest x1 35.6 us: coarsen(): return source.reshape(rows_out, COARSE, cols_out, COARSE).mean(axis=(1, 3))]
    all_to_all x3 -> x4, blocking collectives: 132 us -> 71.2 us  [exchange(): return lax.all_to_all(x, axes, split_axis=0, concat_axis=0, tiled=True)]
    all_to_all x15 -> x4, starting transfers between devices: 72.5 us -> 20.8 us  [exchange(): return lax.all_to_all(x, axes, split_axis=0, concat_axis=0, tiled=True)]
    all_to_all x20 -> x0, local copies, waits for them, and re-layouts: 45.6 us -> none  [the longest x6 15.4 us: inverse(): lax.all_to_all(line_real, ('row', 'col'), split_axis=2, concat_axis=1, ti...]
  transfers between devices with their start and end apart: 19 -> 12, of which waited for: 12 -> 5; matrix products, arithmetic and copies ran while one was open for 22% -> 15% of each run, Pallas kernels for 0% -> 0%
where the time goes in v1:
time: 312 us; the launch traced here: 307 us
  Pallas kernels  81.4 us (26%)
  waiting for transfers between devices  72.2 us (23%)
  blocking collectives  71.2 us (23%)
  other arithmetic  33.2 us (11%)
  starting transfers between devices  29.8 us (10%)
  local copies, waits for them, and re-layouts  17.7 us (6%)
    all_to_all x4, blocking collectives, exchange(): return lax.all_to_all(x, axes, split_axis=0, concat_axis=0, tiled=True)  71.2 us
    all_to_all x4, waiting for transfers between devices, exchange(): return lax.all_to_all(x, axes, split_axis=0, concat_axis=0, tiled=True)  65.7 us
    pallas_call x9, Pallas kernels, run(): pl.pallas_call(kernel, out_shape=shapes, in_specs=specs, out_specs=[vmem]...  62.1 us
    all_to_all x4, starting transfers between devices, exchange(): return lax.all_to_all(x, axes, split_axis=0, concat_axis=0, tiled=True)  20.8 us
    pallas_call x1, Pallas kernels, local(): pl.pallas_call(functools.partial(flow_kernel, levels), grid=(levels,), ou...  19.4 us
    ppermute x8, starting transfers between devices, shift(): lax.ppermute(x, axis, [(i, (i + step) % peers) for i in range(peers)])  9.04 us
    cos x1, other arithmetic, make_tables(): x_inv = parts(jnp.concatenate([jnp.cos(angle), jnp.sin(angle)], axis=1))  8.39 us
    cos x1, other arithmetic, make_tables(): x_fwd = parts(jnp.concatenate([jnp.cos(angle), jnp.sin(angle)], axis=2))  8.19 us
  transfers between devices with their start and end apart: 12, of which 5 were waited for; matrix products, arithmetic and copies ran while one was open for 15% of the time, Pallas kernels for 0%

profile of v1, /device:TPU:3, one launch (start us, length us, event | category | flops | bytes accessed | tf_op | source)
XLA Modules:
  0.0 306.5 jit_solution(14277580530741124346)
XLA Ops:
  0.6 2.5 pack.1
  3.1 4.5 %all-to-all-start = ((f32[8,256,128]{2,1,0:T(8,128)}), f32[8,256,128]{2,1,0:T(8,128)S(1)}, u32[]{:S(2)}, u32[]{:S(2)}) async-start(f32[8,256,128]{2,1,0:T(8,128)} %pack.1), calls=%async_computation | async-start | bytes 2097152 | tf_op jit(solution)/shard_map/all_to_all | solution.py:489
  7.7 3.1 %fusion.23 = (f32[8,96,256]{2,1,0:T(8,128)S(1)}, f32[8,96,256]{2,1,0:T(8,128)S(1)}) fusion(s32[256]{0:T(256)S(1)} %bitcast.33, s32[8,96]{1,0:T(8,128)S(1)} %bitcast.28), kind=kLoop, calls=%fused_computation.55 | loop fusion | flops 2752512 | bytes 1576960 | tf_op jit(solution)/shard_map/cos | solution.py:456
  12.3 9.2 %all-to-all-done.in_ref = f32[8,256,128]{2,1,0:T(8,128)S(1)} async-done(((f32[8,256,128]{2,1,0:T(8,128)}), f32[8,256,128]{2,1,0:T(8,128)S(1)}, u32[]{:S(2)}, u32[]{:S(2)}) %all-to-all-start) | async-done | bytes 1048608 | tf_op jit(solution)/shard_map/all_to_all | solution.py:489
  22.5 4.6 %y0.1 = (f32[32,48,128]{2,1,0:T(8,128)}, f32[8,128,128]{2,1,0:T(8,128)}) custom-call(f32[8,256,128]{2,1,0:T(8,128)} %copy-done.1, bf16[8,96,512]{2,1,0:T(8,128)(2,1)} %get-tuple-element.64.hi_ref.fh, bf16[8,96,512]{2,1,0:T(8,128)(2,1)} %get-tuple-element.63.lo_ref.fl), custom_call_target="tpu_custom_call" | custom-call | tf_op jit(solution)/shard_map/y0/pallas_call | solution.py:475
  27.0 5.8 %all-to-all-start.1 = ((f32[32,48,128]{2,1,0:T(8,128)}), f32[32,48,128]{2,1,0:T(8,128)S(1)}, u32[]{:S(2)}, u32[]{:S(2)}) async-start(f32[32,48,128]{2,1,0:T(8,128)} %get-tuple-element.30), calls=%async_computation.1 | async-start | bytes 1572864 | tf_op jit(solution)/shard_map/all_to_all | solution.py:489
  33.5 8.2 %fusion.16 = (f32[4,512,256]{2,1,0:T(8,128)S(1)}, f32[4,512,256]{2,1,0:T(8,128)S(1)}) fusion(s32[512]{0:T(512)S(1)} %bitcast.31, s32[4,256]{1,0:T(4,128)S(1)} %bitcast.27), kind=kLoop, calls=%fused_computation.48 | loop fusion | flops 7340032 | bytes 4200448 | tf_op jit(solution)/shard_map/cos | solution.py:463
  41.7 8.4 %fusion.14 = (f32[4,256,512]{2,1,0:T(8,128)S(1)}, f32[4,256,512]{2,1,0:T(8,128)S(1)}) fusion(s32[512]{0:T(512)S(1)} %bitcast.30, s32[4,256]{1,0:T(4,128)S(1)} %bitcast.26), kind=kLoop, calls=%fused_computation.46 | loop fusion | flops 7340032 | bytes 4200448 | tf_op jit(solution)/shard_map/cos | solution.py:465
  50.1 3.9 %fusion = (bf16[4,512,512]{2,1,0:T(8,128)(2,1)}, bf16[4,512,512]{2,1,0:T(8,128)(2,1)}, bf16[4,512,512]{2,1,0:T(8,128)(2,1)}, bf16[4,512,512]{2,1,0:T(8,128)(2,1)}) fusion(f32[4,512,256]{2,1,0:T(8,128)S(1)} %get-tuple-element.72, f32[4,512,256]{2,1,0:T(8,128)S(1)} %get-tuple-element.71, f32[4,256,512]{2,1,0:T(8,128)S(1)} %get-tuple-element.70, ...), kind=kLoop, calls=%fused_computation.4 | loop fusion | flops 10485760 | bytes 16777216 | tf_op jit(solution)/shard_map/convert_element_type | solution.py:443
  55.0 11.6 %x7.1 = f32[32,168,128]{2,1,0:T(8,128)} custom-call(s32[2]{0:T(128)} %pad_add_fusion.place_ref, f32[32,48,128]{2,1,0:T(8,128)} %copy-done.2, bf16[4,512,512]{2,1,0:T(8,128)(2,1)} %get-tuple-element.60.fh, bf16[4,512,512]{2,1,0:T(8,128)(2,1)} %get-tuple-element.59.fl, bf16[4,512,512]{2,1,0:T(8,128)(2,1)} %get-tuple-element.77.ih, ...), custom_call_target="tpu_custom_call" | custom-call | tf_op jit(solution)/shard_map/x7/pallas_call | solution.py:475
  66.6 6.0 %all-to-all-start.2 = ((f32[32,168,128]{2,1,0:T(8,128)}), f32[32,168,128]{2,1,0:T(8,128)S(1)}, u32[]{:S(2)}, u32[]{:S(2)}) async-start(f32[32,168,128]{2,1,0:T(8,128)} %x7.1), calls=%async_computation.2 | async-start | bytes 5505024 | tf_op jit(solution)/shard_map/all_to_all | solution.py:489
  72.6 4.1 %fusion.21 = (f32[8,256,96]{2,1,0:T(8,128)S(1)}, f32[8,256,96]{2,1,0:T(8,128)S(1)}) fusion(s32[256]{0:T(256)S(1)} %bitcast.32, s32[8,96]{1,0:T(8,128)S(1)} %bitcast.29), kind=kLoop, calls=%fused_computation.53 | loop fusion | flops 2752512 | bytes 1576960 | tf_op jit(solution)/shard_map/cos | solution.py:458
  76.8 2.1 fusion.2
  78.8 56.5 %all-to-all-done.2.buf_ref = f32[32,168,128]{2,1,0:T(8,128)S(1)} async-done(((f32[32,168,128]{2,1,0:T(8,128)}), f32[32,168,128]{2,1,0:T(8,128)S(1)}, u32[]{:S(2)}, u32[]{:S(2)}) %all-to-all-start.2) | async-done | bytes 2752544 | tf_op jit(solution)/shard_map/all_to_all | solution.py:489
  136.9 12.6 %y1.1 = (f32[32,24,128]{2,1,0:T(8,128)}, f32[8,128,128]{2,1,0:T(8,128)}, f32[8,128,128]{2,1,0:T(8,128)}, f32[8,128,128]{2,1,0:T(8,128)}, f32[8,128,128]{2,1,0:T(...) custom-call(f32[32,168,128]{2,1,0:T(8,128)} %copy-done, f32[8,128,128]{2,1,0:T(8,128)} %get-tuple-element.35.height_ref, ...), custom_call_target="tpu_custom_call" | custom-call | tf_op jit(solution)/shard_map/y1/pallas_call | solution.py:475
  149.5 15.6 %all_to_all.40.in_ref = f32[32,24,128]{2,1,0:T(8,128)} all-to-all(f32[32,24,128]{2,1,0:T(8,128)} %get-tuple-element.38), channel_id=1, replica_groups=mesh['row'=8,'col'=4] {'row','col'}, dimensions={0} | all-to-all | bytes 786432 | tf_op jit(solution)/shard_map/all_to_all | solution.py:489
  165.1 8.4 %x2.1 = f32[32,48,128]{2,1,0:T(8,128)} custom-call(s32[2]{0:T(128)} %pad_add_fusion.place_ref, f32[32,24,128]{2,1,0:T(8,128)} %all_to_all.40.in_ref, bf16[4,512,512]{2,1,0:T(8,128)(2,1)} %get-tuple-element.60.fh, bf16[4,512,512]{2,1,0:T(8,128)(2,1)} %get-tuple-element.59.fl, bf16[4,512,512]{2,1,0:T(8,128)(2,1)} %get-tuple-element.77.ih, ...), custom_call_target="tpu_custom_call" | custom-call | tf_op jit(solution)/shard_map/x2/pallas_call | solution.py:475
  173.5 24.1 %all_to_all.41.buf_ref = f32[32,48,128]{2,1,0:T(8,128)} all-to-all(f32[32,48,128]{2,1,0:T(8,128)} %x2.1), channel_id=1, replica_groups=mesh['row'=8,'col'=4] {'row','col'}, dimensions={0} | all-to-all | bytes 1572864 | tf_op jit(solution)/shard_map/all_to_all | solution.py:489
  197.6 6.2 %y2.1 = (f32[32,24,128]{2,1,0:T(8,128)}, f32[8,128,128]{2,1,0:T(8,128)}) custom-call(f32[32,48,128]{2,1,0:T(8,128)} %all_to_all.41.buf_ref, f32[8,128,128]{2,1,0:T(8,128)} %get-tuple-element.35.height_ref, f32[8,128,128]{2,1,0:T(8,128)} %get-tuple-element.39.vertical_in, f32[8,128,128]{2,1,0:T(8,128)} %get-tuple-element.40.third_in, ...), custom_call_target="tpu_custom_call" | custom-call | tf_op jit(solution)/shard_map/y2/pallas_call | solution.py:475
  203.8 15.8 %all_to_all.42.in_ref = f32[32,24,128]{2,1,0:T(8,128)} all-to-all(f32[32,24,128]{2,1,0:T(8,128)} %get-tuple-element.41), channel_id=1, replica_groups=mesh['row'=8,'col'=4] {'row','col'}, dimensions={0} | all-to-all | bytes 786432 | tf_op jit(solution)/shard_map/all_to_all | solution.py:489
  219.6 8.3 %x1.1 = f32[32,24,128]{2,1,0:T(8,128)} custom-call(s32[2]{0:T(128)} %pad_add_fusion.place_ref, f32[32,24,128]{2,1,0:T(8,128)} %all_to_all.42.in_ref, bf16[4,512,512]{2,1,0:T(8,128)(2,1)} %get-tuple-element.60.fh, bf16[4,512,512]{2,1,0:T(8,128)(2,1)} %get-tuple-element.59.fl, bf16[4,512,512]{2,1,0:T(8,128)(2,1)} %get-tuple-element.77.ih, ...), custom_call_target="tpu_custom_call" | custom-call | tf_op jit(solution)/shard_map/x1/pallas_call | solution.py:475
  227.9 15.8 %all_to_all.43.buf_ref = f32[32,24,128]{2,1,0:T(8,128)} all-to-all(f32[32,24,128]{2,1,0:T(8,128)} %x1.1), channel_id=1, replica_groups=mesh['row'=8,'col'=4] {'row','col'}, dimensions={0} | all-to-all | bytes 786432 | tf_op jit(solution)/shard_map/all_to_all | solution.py:489
  243.6 4.9 %y3.1 = f32[8,320,128]{2,1,0:T(8,128)} custom-call(f32[32,24,128]{2,1,0:T(8,128)} %all_to_all.43.buf_ref, f32[8,128,128]{2,1,0:T(8,128)} %get-tuple-element.42.vertical_in, f32[8,128,128]{2,1,0:T(8,128)} %get-tuple-element.43.slope_ref, f32[8,128,128]{2,1,0:T(8,128)} %get-tuple-element.44.rate_ref, f32[8,128,128]{2,1,0:T(8,128)} %get-tuple-element.45.energy_ref, ...), custom_call_target="tpu_custom_call" | custom-call | tf_op jit(solution)/shard_map/y3/pallas_call | solution.py:475
  248.5 4.4 %all-to-all-start.7 = ((f32[8,320,128]{2,1,0:T(8,128)}), f32[8,320,128]{2,1,0:T(8,128)}, u32[]{:S(2)}, u32[]{:S(2)}) async-start(f32[8,320,128]{2,1,0:T(8,128)} %y3.1), calls=%async_computation.7 | async-start | bytes 2621440 | tf_op jit(solution)/shard_map/all_to_all | solution.py:489
  252.9 5.5 %fusion.24 = (f32[3,16,128,1]{3,2,1,0:T(8,128)}, f32[3,16,128,1]{3,2,1,0:T(8,128)S(1)}) fusion(f32[3,16,128,256]{3,2,1,0:T(8,128)} %next_ref.1), kind=kLoop, calls=%fused_computation.75 | loop fusion | bytes 98304 | tf_op jit(solution)/shard_map/slice | solution.py:514
  258.4 2.6 copy.21
  267.1 1.8 collective-permute-start
  270.4 3.2 %collective-permute-done.1 = f32[3,16,256]{2,0,1:T(4,128)S(1)} collective-permute-done((f32[3,16,256]{2,0,1:T(4,128)S(1)}, f32[3,16,256]{2,0,1:T(4,128)S(1)}, u32[]{:S(2)}, u32[]{:S(2)}) %collective-permute-start.1) | collective-permute-done | bytes 49184 | tf_op jit(solution)/shard_map/ppermute | solution.py:494
  274.3 2.9 tile.1
  278.0 3.2 %collective-permute-start.7 = (f32[1,128]{1,0:T(1,128)S(1)}, f32[1,128]{1,0:T(1,128)S(1)}, u32[]{:S(2)}, u32[]{:S(2)}) collective-permute-start(f32[1,128]{1,0:T(1,128)S(1)} %get-tuple-element.68), channel_id=1, source_target_pairs={{0,3},{1,0},{2,1},{3,2},{4,7},{5,4},{6,5},{7,6},{8,11},{9,8},{10,9... | collective-permute-start | bytes 1544 | tf_op jit(solution)/shard_map/ppermute | solution.py:494
  283.2 3.2 %collective-permute-done.5 = f32[1,256]{1,0:T(1,128)S(1)} collective-permute-done((f32[1,256]{1,0:T(1,128)S(1)}, f32[1,256]{1,0:T(1,128)S(1)}, u32[]{:S(2)}, u32[]{:S(2)}) %collective-permute-start.5) | collective-permute-done | bytes 1056 | tf_op jit(solution)/shard_map/ppermute | solution.py:494
  286.9 19.4 %flow.1 = f32[3,16,128,256]{3,2,1,0:T(8,128)} custom-call(f32[16,2]{1,0:T(8,128)} %copy.18.decay_ref, f32[3,16,128,256]{3,2,1,0:T(8,128)} %next_ref.1, f32[3,16,128,256]{3,2,1,0:T(8,128)} %next_ref.1, f32[3,16,128,256]{3,2,1,0:T(8,128)} %next_ref.1, f32[16,8,256]{2,1,0:T(8,128)} %pad.16.rows_ref, f32[16,8,128]{2,1,0:T(8,128)} %pad.17.cols_ref, ...), custom_call_target="tpu_custom_call" | custom-call | tf_op jit(solution)/shard_map/flow/pallas_call | solution.py:573
  (47 shorter events, 17.0 us)
Async XLA Ops:
  3.1 18.4 %all-to-all-start = ((f32[8,256,128]{2,1,0:T(8,128)}), f32[8,256,128]{2,1,0:T(8,128)S(1)}, u32[]{:S(2)}, u32[]{:S(2)}) async-start(f32[8,256,128]{2,1,0:T(8,128)} %pack.1), calls=%async_computation | async-start | bytes 2097152 | tf_op jit(solution)/shard_map/all_to_all | solution.py:489
  21.5 1.0 copy-start.1
  27.0 27.0 %all-to-all-start.1 = ((f32[32,48,128]{2,1,0:T(8,128)}), f32[32,48,128]{2,1,0:T(8,128)S(1)}, u32[]{:S(2)}, u32[]{:S(2)}) async-start(f32[32,48,128]{2,1,0:T(8,128)} %get-tuple-element.30), calls=%async_computation.1 | async-start | bytes 1572864 | tf_op jit(solution)/shard_map/all_to_all | solution.py:489
  54.0 0.9 copy-start.2
  66.6 68.8 %all-to-all-start.2 = ((f32[32,168,128]{2,1,0:T(8,128)}), f32[32,168,128]{2,1,0:T(8,128)S(1)}, u32[]{:S(2)}, u32[]{:S(2)}) async-start(f32[32,168,128]{2,1,0:T(8,128)} %x7.1), calls=%async_computation.2 | async-start | bytes 5505024 | tf_op jit(solution)/shard_map/all_to_all | solution.py:489
  135.3 1.5 copy-start
  248.5 25.8 %all-to-all-start.7 = ((f32[8,320,128]{2,1,0:T(8,128)}), f32[8,320,128]{2,1,0:T(8,128)}, u32[]{:S(2)}, u32[]{:S(2)}) async-start(f32[8,320,128]{2,1,0:T(8,128)} %y3.1), calls=%async_computation.7 | async-start | bytes 2621440 | tf_op jit(solution)/shard_map/all_to_all | solution.py:489
  261.1 8.7 %collective-permute-start.2 = (f32[3,16,128]{2,0,1:T(4,128)S(1)}, f32[3,16,128]{2,0,1:T(4,128)S(1)}, u32[]{:S(2)}, u32[]{:S(2)}) collective-permute-start(f32[3,16,128]{2,0,1:T(4,128)S(1)} %bitcast.24), channel_id=1, source_target_pairs={{0,1},{1,2},{2,3},{3,0},{4,5},{5,6},{6,7},{7,4},{8,9},{9,10},{10,1... | collective-permute-start | bytes 73736 | tf_op jit(solution)/shard_map/ppermute | solution.py:494
  264.2 5.6 %collective-permute-start.3 = (f32[3,16,128]{2,0,1:T(4,128)S(1)}, f32[3,16,128]{2,0,1:T(4,128)S(1)}, u32[]{:S(2)}, u32[]{:S(2)}) collective-permute-start(f32[3,16,128]{2,0,1:T(4,128)S(1)} %bitcast.25), channel_id=1, source_target_pairs={{0,3},{1,0},{2,1},{3,2},{4,7},{5,4},{6,5},{7,6},{8,11},{9,8},{10,9... | collective-permute-start | bytes 73736 | tf_op jit(solution)/shard_map/ppermute | solution.py:494
  267.1 3.3 %collective-permute-start = (f32[3,16,256]{2,0,1:T(4,128)S(1)}, f32[3,16,256]{2,0,1:T(4,128)S(1)}, u32[]{:S(2)}, u32[]{:S(2)}) collective-permute-start(f32[3,16,256]{2,0,1:T(4,128)S(1)} %bitcast.22), channel_id=1, source_target_pairs={{0,4},{4,8},{8,12},{12,16},{16,20},{20,24},{24,28},{28,0},{1,5},{5... | collective-permute-start | bytes 147464 | tf_op jit(solution)/shard_map/ppermute | solution.py:494
  269.0 4.6 %collective-permute-start.1 = (f32[3,16,256]{2,0,1:T(4,128)S(1)}, f32[3,16,256]{2,0,1:T(4,128)S(1)}, u32[]{:S(2)}, u32[]{:S(2)}) collective-permute-start(f32[3,16,256]{2,0,1:T(4,128)S(1)} %bitcast.23), channel_id=1, source_target_pairs={{0,28},{4,0},{8,4},{12,8},{16,12},{20,16},{24,20},{28,24},{1,29},{... | collective-permute-start | bytes 147464 | tf_op jit(solution)/shard_map/ppermute | solution.py:494
  277.9 4.5 %collective-permute-start.6 = (f32[1,128]{1,0:T(1,128)S(1)}, f32[1,128]{1,0:T(1,128)S(1)}, u32[]{:S(2)}, u32[]{:S(2)}) collective-permute-start(f32[1,128]{1,0:T(1,128)S(1)} %get-tuple-element.67), channel_id=1, source_target_pairs={{0,1},{1,2},{2,3},{3,0},{4,5},{5,6},{6,7},{7,4},{8,9},{9,10},{10,1... | collective-permute-start | bytes 1544 | tf_op jit(solution)/shard_map/ppermute | solution.py:494
  278.0 4.4 %collective-permute-start.7 = (f32[1,128]{1,0:T(1,128)S(1)}, f32[1,128]{1,0:T(1,128)S(1)}, u32[]{:S(2)}, u32[]{:S(2)}) collective-permute-start(f32[1,128]{1,0:T(1,128)S(1)} %get-tuple-element.68), channel_id=1, source_target_pairs={{0,3},{1,0},{2,1},{3,2},{4,7},{5,4},{6,5},{7,6},{8,11},{9,8},{10,9... | collective-permute-start | bytes 1544 | tf_op jit(solution)/shard_map/ppermute | solution.py:494
  281.9 1.2 collective-permute-start.4
  282.4 3.9 %collective-permute-start.5 = (f32[1,256]{1,0:T(1,128)S(1)}, f32[1,256]{1,0:T(1,128)S(1)}, u32[]{:S(2)}, u32[]{:S(2)}) collective-permute-start(f32[1,256]{1,0:T(1,128)S(1)} %get-tuple-element.66), channel_id=1, source_target_pairs={{0,28},{4,0},{8,4},{12,8},{16,12},{20,16},{24,20},{28,24},{1,29},{... | collective-permute-start | bytes 3080 | tf_op jit(solution)/shard_map/ppermute | solution.py:494

commit v2 on v1

v2 whole, which is shorter than its diff:
```python
import functools
import math

import jax
import jax.numpy as jnp
from jax import lax
from jax.experimental import pallas as pl
from jax.experimental.pallas import tpu as pltpu
from jax.sharding import PartitionSpec as P

COARSE = 2
GRAVITY = 1.0
SURFACE_STEP = 0.05
FLOW_STEP = 0.5
VISCOSITY = 0.2
DECAY_RATE = 0.05

F32 = jnp.float32
BF16 = jnp.bfloat16
MIB = 1024 * 1024


def round_up(value, step):
    return -(-value // step) * step


class Plan:
    def __init__(self, rows, cols, tile):
        self.R, self.C = rows, cols
        self.NYL, self.NXL = tile
        self.NY, self.NX = rows * self.NYL, cols * self.NXL
        self.XC = self.NXL // rows
        self.Q = max(1, 128 // self.XC)
        self.NYF = self.NYL // self.Q
        self.W = self.Q * self.XC
        self.KEPT_Y = self.NY // 3 + 1
        self.KEPT_X = self.NX // 3 + 1
        self.M = round_up(-(-(-(-self.KEPT_Y // rows)) // cols), 8)
        self.KY = cols * self.M
        self.J = round_up(-(-self.KEPT_X // cols), 128)
        self.L2 = 2 * self.XC
        self.PEERS = rows * cols
        self.NYC, self.NXC = self.NYF // COARSE, self.W // COARSE


def split(x):
    hi = x.astype(BF16)
    return hi, (x - hi.astype(F32)).astype(BF16)


def dot(a, b, flipped=False):
    dims = (((1,), (1 if flipped else 0,)), ((), ()))
    return lax.dot_general(a, b, dims, preferred_element_type=F32)


def cat(parts, axis):
    return parts[0] if len(parts) == 1 else jnp.concatenate(parts, axis=axis)


def turn(numer, denom):
    numer %= denom
    exact = {0: (1.0, 0.0), 1: (0.0, 1.0), 2: (-1.0, 0.0), 3: (0.0, -1.0)}
    if 4 * numer % denom == 0:
        return exact[4 * numer // denom]
    angle = 2.0 * math.pi * numer / denom
    return math.cos(angle), math.sin(angle)


def combine(terms):
    total = None
    for factor, value in terms:
        if factor == 0.0:
            continue
        if total is None:
            total = value if factor == 1.0 else (-value if factor == -1.0 else factor * value)
        elif factor == 1.0:
            total = total + value
        elif factor == -1.0:
            total = total - value
        else:
            total = total + factor * value
    return total


def mirrored(index, count):
    if index == 0 or 2 * index == count:
        return ((index, 1.0),)
    return ((index, 1.0), (count - index, -1.0))


def unfold(x, plan):
    return cat([x[:, h * plan.XC : (h + 1) * plan.XC] for h in range(plan.Q)], 0)


def fold(x, plan):
    return cat([x[h * plan.NYF : (h + 1) * plan.NYF] for h in range(plan.Q)], 1)


def swap_halves(x, half):
    if 2 * half == 128:
        return pltpu.roll(x, half, 1)
    return jnp.concatenate([x[:, half:], x[:, :half]], axis=1)


def table_rows(table, rhs):
    rows = table.shape[0] // 2
    both = dot(table, rhs[0])
    return both[:rows] + (both[rows:] + dot(table[:rows], rhs[1]))


def y_forward(plan, blocks, field, tab, out_ref):
    for k0 in range(plan.R // 2 + 1):
        even = combine([(turn(k0 * r, plan.R)[0], blocks[r]) for r in range(plan.R)])
        odd = combine([(turn(k0 * r, plan.R)[1], blocks[r]) for r in range(plan.R)])
        even = split(unfold(even, plan))
        if odd is None:
            odd = tuple(jnp.zeros_like(e) for e in even)
        else:
            odd = split(unfold(odd, plan))
        for k, sign in mirrored(k0, plan.R):
            if sign > 0:
                pos, neg = odd, [-o for o in odd]
            else:
                pos, neg = [-o for o in odd], odd
            rhs = [
                jnp.concatenate(
                    [
                        jnp.concatenate([even[i], pos[i]], axis=1),
                        jnp.concatenate([neg[i], even[i]], axis=1),
                    ],
                    axis=0,
                )
                for i in range(2)
            ]
            lines = table_rows(tab[k], rhs)
            for c in range(plan.C):
                out_ref[k * plan.C + c, field * plan.M : (field + 1) * plan.M, :] = lines[
                    c * plan.M : (c + 1) * plan.M
                ]


def y_inverse(plan, buf_ref, fields, tab, work_ref):
    L2, M, C = plan.L2, plan.M, plan.C
    lane = lax.broadcasted_iota(jnp.int32, (1, L2), 1)
    flip = jnp.where(lane < plan.XC, 1.0, -1.0).astype(F32)
    for k0 in range(plan.R // 2 + 1):
        total = None
        for k, sign in mirrored(k0, plan.R):
            tops, bottoms = [], []
            for f in range(fields):
                lines = cat(
                    [buf_ref[k * C + c, f * M : (f + 1) * M, :] for c in range(C)], 0
                )
                tops.append(lines)
                bottoms.append(swap_halves(lines, plan.XC) * flip)
            rhs = split(jnp.concatenate([cat(tops, 1), cat(bottoms, 1)], axis=0))
            part = table_rows(tab[k], rhs)
            if sign > 0:
                total = part
            else:
                total = total + part * cat([flip] * fields, 1)
        work_ref[k0] = total


def y_block(plan, work_ref, field, r):
    L2 = plan.L2
    lane = lax.broadcasted_iota(jnp.int32, (1, L2), 1)
    total = None
    for k0 in range(plan.R // 2 + 1):
        c, s = turn(k0 * r, plan.R)
        factor = jnp.where(lane < plan.XC, c, s).astype(F32)
        part = work_ref[k0, :, field * L2 : (field + 1) * L2] * factor
        total = part if total is None else total + part
    if L2 == 128 and plan.Q == 2:
        both = total + pltpu.roll(total, plan.XC, 1)
        return jnp.where(lane < plan.XC, both[: plan.NYF], both[plan.NYF :])
    return fold(total[:, : plan.XC] + total[:, plan.XC :], plan)


def pack_kernel(plan, potential_ref, height_ref, out_ref):
    for r in range(plan.R):
        for f, ref in enumerate((potential_ref, height_ref)):
            out_ref[r, f * plan.NYF : (f + 1) * plan.NYF, :] = fold(
                ref[:, r * plan.XC : (r + 1) * plan.XC], plan
            )


def first_kernel(plan, in_ref, yf, out_ref, height_ref):
    for f in range(2):
        blocks = [in_ref[r, f * plan.NYF : (f + 1) * plan.NYF, :] for r in range(plan.R)]
        y_forward(plan, blocks, f, yf, out_ref)
    for r in range(plan.R):
        height_ref[r] = in_ref[r, plan.NYF :, :]


def stacked(pair, table_hi, table_lo, flipped=False):
    hi = cat([p[0] for p in pair], 0)
    lo = cat([p[1] for p in pair], 0)
    rows = hi.shape[0]
    both = dot(jnp.concatenate([hi, lo], axis=0), table_hi, flipped)
    total = both[:rows] + (both[rows:] + dot(hi, table_lo, flipped))
    rows = pair[0][0].shape[0]
    return [total[i * rows : (i + 1) * rows] for i in range(len(pair))]


def x_kernel(
    plan, sources, wanted, place_ref, in_ref, fh, fl, out_ref, u_ref,
):
    R, C, M, J, XC, NXL = plan.R, plan.C, plan.M, plan.J, plan.XC, plan.NXL
    fields, outs = len(sources), len(wanted)
    rows = fields * M
    lines = []
    for c in range(C):
        parts_of = []
        for h in range(2):
            for f in sources:
                parts_of.append(
                    cat(
                        [
                            in_ref[r * C + c, f * M : (f + 1) * M, h * XC : (h + 1) * XC]
                            for r in range(R)
                        ],
                        1,
                    )
                )
        lines.append(jnp.concatenate(parts_of, axis=0))
    row_k0, row_k1 = place_ref[0], place_ref[1]
    ky_index = R * (row_k1 + lax.broadcasted_iota(jnp.int32, (M, J), 0)) + row_k0
    ky = ky_index.astype(F32) * (2.0 * math.pi / plan.NY)
    y_weight = jnp.where(
        ky_index == 0, 1.0, jnp.where(ky_index < plan.KEPT_Y, 2.0, 0.0)
    ).astype(F32)
    slot = 0
    slots = []
    for j0 in range(C // 2 + 1):
        pair = [split(combine([(turn(j0 * c, C)[0], lines[c]) for c in range(C)]))]
        odd = combine([(turn(j0 * c, C)[1], lines[c]) for c in range(C)])
        if odd is not None:
            pair.append(split(odd))
        u_sum = v_sum = None
        for j, sign in mirrored(j0, C):
            found = stacked(pair, fh[j], fl[j])
            p_all, q_all = found[0][:, :J], found[0][:, J:]
            if odd is not None:
                p_all = p_all - sign * found[1][:, J:]
                q_all = q_all + sign * found[1][:, :J]
            kx_index = C * lax.broadcasted_iota(jnp.int32, (M, J), 1) + j
            kx = kx_index.astype(F32) * (2.0 * math.pi / plan.NX)
            x_weight = jnp.where(
                kx_index == 0, 1.0, jnp.where(kx_index < plan.KEPT_X, 2.0, 0.0)
            ).astype(F32)
            weight = x_weight * y_weight * (1.0 / (plan.NX * plan.NY))
            size = jnp.sqrt(kx * kx + ky * ky)
            coef = []
            for f in range(fields):
                top, low = slice(f * M, (f + 1) * M), slice(rows + f * M, rows + (f + 1) * M)
                coef.append(
                    (
                        p_all[top] * weight,
                        q_all[top] * weight,
                        p_all[low] * weight,
                        q_all[low] * weight,
                    )
                )
            tops, lows = [], []
            for f, kind in wanted:
                cc, cs, sc, ss = coef[f]
                if kind == "dx":
                    new = (kx * cs, -kx * cc, kx * ss, -kx * sc)
                elif kind == "dy":
                    new = (ky * sc, ky * ss, -ky * cc, -ky * cs)
                else:
                    factor = size
                    for _ in range(kind - 1):
                        factor = factor * size
                    new = (factor * cc, factor * cs, factor * sc, factor * ss)
                tops.append((new[0], new[1]))
                lows.append((new[2], new[3]))
            p_new = split(cat([t[0] for t in tops] + [t[0] for t in lows], 0))
            q_new = split(cat([t[1] for t in tops] + [t[1] for t in lows], 0))
            pair_back = [[jnp.concatenate([p_new[i], q_new[i]], axis=1) for i in range(2)]]
            if odd is not None:
                pair_back.append(
                    [jnp.concatenate([q_new[i], -p_new[i]], axis=1) for i in range(2)]
                )
            found = stacked(pair_back, fh[j], fl[j], True)
            u_sum = found[0] if u_sum is None else u_sum + found[0]
            if odd is not None:
                v_sum = found[1] if v_sum is None else v_sum - found[1]
        u_ref[slot] = u_sum
        slots.append((j0, slot, None if v_sum is None else slot + 1))
        if v_sum is not None:
            u_ref[slot + 1] = v_sum
        slot += 1 if v_sum is None else 2
    half = outs * M
    for c in range(C):
        terms = []
        for j0, u_slot, v_slot in slots:
            cs, sn = turn(j0 * c, C)
            terms.append((cs, u_slot))
            if v_slot is not None:
                terms.append((sn, v_slot))
        for r in range(0, R):
            lanes = slice(r * XC, (r + 1) * XC)
            top = combine([(a, u_ref[s, :half, lanes]) for a, s in terms if a != 0.0])
            low = combine([(a, u_ref[s, half:, lanes]) for a, s in terms if a != 0.0])
            out_ref[r * C + c] = jnp.concatenate([top, low], axis=1)


def second_kernel(
    plan, buf_ref, height_ref, yi, yf, out_ref, vert_ref, work_ref
):
    y_inverse(plan, buf_ref, 1, yi, work_ref)
    blocks = []
    for r in range(plan.R):
        vert = y_block(plan, work_ref, 0, r)
        vert_ref[r] = vert
        blocks.append(-height_ref[r] * vert)
    y_forward(plan, blocks, 0, yf, out_ref)


def fields_kernel(
    plan, buf_ref, height_ref, vert_ref, yi,
    vertical_ref, third_ref, slope_ref, rate_ref, energy_ref, coarse_ref,
    work_ref,
):
    y_inverse(plan, buf_ref, 6, yi, work_ref)
    pool_y, pool_x = pools(plan.NYC, plan.NYF, plan.W, plan.NXC)
    for r in range(plan.R):
        height = height_ref[r]
        curve, cube, pot_dx, pot_dy, height_dx, height_dy = [
            y_block(plan, work_ref, f, r) for f in range(6)
        ]
        square = 0.5 * height * height
        vertical_ref[r] = vert_ref[r] + height * curve + square * cube
        third_ref[r] = -square * curve
        slope_ref[r] = height_dx * height_dx + height_dy * height_dy
        rate_ref[r] = -(height_dx * pot_dx + height_dy * pot_dy)
        energy_ref[r] = -GRAVITY * height - 0.5 * (pot_dx * pot_dx + pot_dy * pot_dy)
        coarse_ref[r] = jnp.concatenate(
            [pooled(pot_dx, pool_y, pool_x), pooled(pot_dy, pool_y, pool_x)], axis=1
        )


def third_kernel(
    plan, buf_ref, height_ref, vertical_in, third_in, yi, yf, out_ref, vertical_ref,
    work_ref,
):
    y_inverse(plan, buf_ref, 2, yi, work_ref)
    blocks = []
    for r in range(plan.R):
        height = height_ref[r]
        vert, curve = [y_block(plan, work_ref, f, r) for f in range(2)]
        vertical_ref[r] = vertical_in[r] + vert + height * curve
        blocks.append(third_in[r] - height * vert)
    y_forward(plan, blocks, 0, yf, out_ref)


def rates_kernel(
    plan, buf_ref, vertical_in, slope_ref, rate_ref, energy_ref, yi, out_ref,
    work_ref,
):
    y_inverse(plan, buf_ref, 1, yi, work_ref)
    N = plan.NYF
    for r in range(plan.R):
        vertical = vertical_in[r] + y_block(plan, work_ref, 0, r)
        lift = (1.0 + slope_ref[r]) * vertical
        out_ref[r, :N, :] = rate_ref[r] + lift
        out_ref[r, N : 2 * N, :] = energy_ref[r] + 0.5 * lift * vertical


def pools(rows_out, rows_in, cols_in, cols_out):
    def pool(shape, out_dim):
        i = lax.broadcasted_iota(jnp.int32, shape, out_dim)
        k = lax.broadcasted_iota(jnp.int32, shape, 1 - out_dim)
        return jnp.where((k >= COARSE * i) & (k < COARSE * (i + 1)), 1.0 / COARSE, 0.0).astype(BF16)

    return pool((rows_out, rows_in), 0), pool((cols_in, cols_out), 1)


def pooled(x, pool_y, pool_x):
    hi, lo = split(x)
    low = (x - hi.astype(F32) - lo.astype(F32)).astype(BF16)
    lines = dot(hi, pool_x) + (dot(lo, pool_x) + dot(low, pool_x))
    hi, lo = split(lines)
    low = (lines - hi.astype(F32) - lo.astype(F32)).astype(BF16)
    return dot(pool_y, hi) + (dot(pool_y, lo) + dot(pool_y, low))


def current_kernel(plan, in_ref, u_ref, v_ref):
    XH = plan.XC // COARSE
    for f, ref in enumerate((u_ref, v_ref)):
        for h in range(plan.Q):
            base = f * plan.NXC + h * XH
            ref[h * plan.NYC : (h + 1) * plan.NYC, :] = cat(
                [in_ref[r, :, base : base + XH] for r in range(plan.R)], 1
            )


def edges_kernel(in_ref, top_ref, bottom_ref, west_ref, east_ref):
    for ref in (top_ref, bottom_ref, west_ref, east_ref):
        ref[...] = jnp.zeros_like(ref)
    for q in range(3):
        x = in_ref[q, 0]
        top_ref[0, q : q + 1] = x[:1]
        bottom_ref[0, q : q + 1] = x[-1:]
        west_ref[0, q : q + 1] = jnp.transpose(x[:, :128])[:1]
        east_ref[0, q : q + 1] = jnp.transpose(x[:, -128:])[-1:]


def tile_kernel(
    plan, in_ref, height_ref, rate_ref, energy_ref, pressure_ref, top_ref, bottom_ref, west_ref, east_ref
):
    R, Q, XC, N = plan.R, plan.Q, plan.XC, plan.NYF
    for f, ref in enumerate((rate_ref, energy_ref)):
        for h in range(Q):
            ref[h * N : (h + 1) * N, :] = cat(
                [in_ref[r, f * N : (f + 1) * N, h * XC : (h + 1) * XC] for r in range(R)], 1
            )
    pool_y, pool_x = pools(plan.NYL // COARSE, plan.NYL, plan.NXL, plan.NXL // COARSE)
    pressure = GRAVITY * pooled(height_ref[...] + SURFACE_STEP * rate_ref[...], pool_y, pool_x)
    pressure_ref[...] = pressure
    top_ref[...] = pressure[:8]
    bottom_ref[...] = pressure[-8:]
    west_ref[...] = jnp.transpose(pressure[:, :128])[:8]
    east_ref[...] = jnp.transpose(pressure[:, -128:])[-8:]


def around(x, south, north, west, east):
    ny, nx = x.shape
    lane = lax.broadcasted_iota(jnp.int32, (ny, nx), 1)
    line = lax.broadcasted_iota(jnp.int32, (ny, nx), 0)
    return (
        jnp.where(lane == nx - 1, east, pltpu.roll(x, nx - 1, 1)),
        jnp.where(lane == 0, west, pltpu.roll(x, 1, 1)),
        jnp.where(line == ny - 1, north, pltpu.roll(x, ny - 1, 0)),
        jnp.where(line == 0, south, pltpu.roll(x, 1, 0)),
    )


def flow_kernel(
    decay_ref, prev_ref, cur_ref, next_ref, south_ref, north_ref, west_ref, east_ref,
    u_ref, v_ref, out_ref,
):
    level = pl.program_id(0)
    west_cols, east_cols = jnp.transpose(west_ref[0]), jnp.transpose(east_ref[0])
    top_u, top_v = u_ref[...], v_ref[...]
    is_top = level == 0

    def derivs(q, top):
        mid = cur_ref[q, 0]
        east, west, north, south = around(
            mid,
            south_ref[0, q : q + 1, :],
            north_ref[0, q : q + 1, :],
            west_cols[:, q : q + 1],
            east_cols[:, q : q + 1],
        )
        above = jnp.where(is_top, top, prev_ref[q, 0])
        below = next_ref[q, 0]
        lap = (east + west) + (north + south) + (above + below) - 6.0 * mid
        return mid, 0.5 * (east - west), 0.5 * (north - south), 0.5 * (above - below), lap

    u, u_dx, u_dy, u_dz, u_lap = derivs(0, top_u)
    v, v_dx, v_dy, v_dz, v_lap = derivs(1, top_v)
    w, w_dx, w_dy, w_dz, w_lap = derivs(2, jnp.zeros_like(top_u))
    drift_u = top_u * decay_ref[level, 0]
    drift_v = top_v * decay_ref[level, 0]
    vort_x = w_dy - v_dz
    vort_y = u_dz - w_dx
    vort_z = v_dx - u_dy

    def advance(mid, dx, dy, dz, lap, force):
        return mid + FLOW_STEP * (VISCOSITY * lap + force - (u * dx + v * dy + w * dz))

    out_ref[0, 0] = advance(u, u_dx, u_dy, u_dz, u_lap, drift_v * vort_z)
    out_ref[1, 0] = advance(v, v_dx, v_dy, v_dz, v_lap, -drift_u * vort_z)
    out_ref[2, 0] = advance(w, w_dx, w_dy, w_dz, w_lap, drift_u * vort_y - drift_v * vort_x)


def load_kernel(
    depth, decay_ref, flow_ref, pressure_ref, south_ref, north_ref, west_ref, east_ref,
    out_ref, x_ref, y_ref,
):
    step = pl.program_id(0)

    @pl.when(step == 0)
    def _():
        east, west, north, south = around(
            pressure_ref[...],
            south_ref[7:8, :],
            north_ref[0:1, :],
            jnp.transpose(west_ref[...])[:, 7:8],
            jnp.transpose(east_ref[...])[:, 0:1],
        )
        x_ref[...] = (0.5 * FLOW_STEP) * (east - west)
        y_ref[...] = (0.5 * FLOW_STEP) * (north - south)

    for l in range(depth):
        load = decay_ref[step * depth + l, 1]
        out_ref[0, l] = flow_ref[0, l] - load * x_ref[...]
        out_ref[1, l] = flow_ref[1, l] - load * y_ref[...]


def parts(table):
    hi = lax.reduce_precision(table, 8, 7)
    return hi.astype(BF16), (table - hi).astype(BF16)


def turns(numbers, places, total):
    numbers, places = lax.optimization_barrier((numbers, places))
    angle = (numbers * places % total).astype(F32) * (2.0 * math.pi / total)
    return lax.optimization_barrier((jnp.cos(angle), jnp.sin(angle)))


def table(coarse, fine, axis):
    return jnp.concatenate(
        [
            coarse[0] * fine[0] - coarse[1] * fine[1],
            coarse[1] * fine[0] + coarse[0] * fine[1],
        ],
        axis=axis,
    )


def make_tables(plan):
    ints = lambda count, *dims: jnp.expand_dims(jnp.arange(count, dtype=jnp.int32), dims)
    R, C, NY, NX = plan.R, plan.C, plan.NY, plan.NX
    coarse = turns(R * ints(plan.KY, 0, 2), ints(plan.NYL, 0, 1), NY)
    fine = turns(ints(R, 1, 2), ints(plan.NYL, 0, 1), NY)
    y_fwd = jnp.concatenate(parts(table(coarse, fine, 2)), axis=1)
    coarse = turns(R * ints(plan.KY, 0, 1), ints(plan.NYL, 0, 2), NY)
    fine = turns(ints(R, 1, 2), ints(plan.NYL, 0, 2), NY)
    y_inv = jnp.concatenate(parts(table(coarse, fine, 2)), axis=1)
    coarse = turns(C * ints(plan.J, 0, 1), ints(plan.NXL, 0, 2), NX)
    fine = turns(ints(C, 1, 2), ints(plan.NXL, 0, 2), NX)
    x_fwd = parts(table(coarse, fine, 2))
    return y_fwd, y_inv, x_fwd


def call(kernel, name, outs, args, smem=0, tables=(), work=(), cost=4.0, limit=12):
    vmem = pl.BlockSpec(memory_space=pltpu.VMEM)
    args = [*args, *tables]
    return pl.pallas_call(
        kernel,
        out_shape=[jax.ShapeDtypeStruct(o, F32) for o in outs],
        in_specs=[pl.BlockSpec(memory_space=pltpu.SMEM)] * smem + [vmem] * (len(args) - smem),
        out_specs=[vmem] * len(outs),
        scratch_shapes=[pltpu.VMEM(w, F32) for w in work],
        compiler_params=pltpu.CompilerParams(vmem_limit_bytes=limit * MIB),
        cost_estimate=priced(cost),
        name=name,
    )(*args)


def priced(microseconds):
    return pl.CostEstimate(
        flops=int(microseconds * 3e8), bytes_accessed=int(microseconds * 1e6), transcendentals=0
    )


def exchange(x, axes):
    return lax.all_to_all(x, axes, split_axis=0, concat_axis=0, tiled=True)


def shift(x, axis, step):
    peers = lax.axis_size(axis)
    return lax.ppermute(x, axis, [(i, (i + step) % peers) for i in range(peers)])


def from_neighbours(top, bottom, west, east):
    return (
        shift(bottom, "row", 1),
        shift(top, "row", -1),
        shift(east, "col", 1),
        shift(west, "col", -1),
    )


def local(surface_height, surface_potential, velocity):
    plan = Plan(lax.axis_size("row"), lax.axis_size("col"), surface_height.shape)
    R, C, M, W, N, L2 = plan.R, plan.C, plan.M, plan.W, plan.NYF, plan.L2
    bind = lambda kernel, *rest: functools.partial(kernel, plan, *rest)
    both = ("row", "col")
    pencil = (R, N, W)
    work = lambda f: (R // 2 + 1, plan.NYL, f * L2)
    spec = lambda f: (plan.PEERS, f * M, L2)

    (packed,) = call(
        bind(pack_kernel), "pack", [(R, 2 * N, W)], [surface_potential, surface_height]
    )
    packed = exchange(packed, "row")

    levels, ny, nx = velocity.shape[1:]
    depth = 4 if levels % 4 == 0 else 1
    block = (3, 1, ny, nx)
    at = lambda step: pl.BlockSpec(
        block, lambda l: (0, jnp.clip(l + step, 0, levels - 1), 0, 0)
    )
    whole = lambda x: pl.BlockSpec(x.shape, lambda l: (0,) * x.ndim)
    per_level = lambda length: pl.BlockSpec((1, 8, length), lambda l: (l, 0, 0))
    smem = pl.BlockSpec(memory_space=pltpu.SMEM)
    edge_specs = [per_level(nx)] * 2 + [per_level(ny)] * 2
    edges = pl.pallas_call(
        edges_kernel,
        grid=(levels,),
        out_shape=[jax.ShapeDtypeStruct((levels, 8, n), F32) for n in (nx, nx, ny, ny)],
        in_specs=[at(0)],
        out_specs=edge_specs,
        compiler_params=pltpu.CompilerParams(vmem_limit_bytes=16 * MIB),
        cost_estimate=priced(5.0),
        name="edges",
    )(velocity)
    edges = from_neighbours(*edges)
    mid = jnp.arange(levels, dtype=F32) + 0.5
    decay = jnp.stack([jnp.exp(-2.0 * DECAY_RATE * mid), jnp.exp(-DECAY_RATE * mid)], axis=1)

    y_fwd, y_inv, x_tables = make_tables(plan)
    place = jnp.stack([lax.axis_index("row"), lax.axis_index("col") * M]).astype(jnp.int32)

    def x_stage(buf, sources, wanted):
        outs = len(wanted)
        slots = C // 2 + 1 + max(0, (C - 1) // 2)
        (out,) = call(
            bind(x_kernel, sources, wanted),
            "x%d" % outs,
            [spec(outs)],
            [place, buf],
            smem=1,
            tables=x_tables,
            work=[(slots, 2 * outs * M, plan.NXL)],
            cost=3.0 + outs,
            limit=10 + 2 * outs,
        )
        return out

    first, height = call(bind(first_kernel), "y0", [spec(2), pencil], [packed], tables=[y_fwd])
    first = exchange(first, both)
    vert = exchange(x_stage(first, (0,), ((0, 1),)), both)
    rest = exchange(
        x_stage(first, (0, 1), ((0, 2), (0, 3), (0, "dx"), (0, "dy"), (1, "dx"), (1, "dy"))),
        both,
    )
    second, vert = call(
        bind(second_kernel), "y1", [spec(1), pencil], [vert, height],
        tables=[y_inv, y_fwd], work=[work(1)],
    )
    second = exchange(second, both)
    vertical, third, slope, rate, energy, coarse = call(
        bind(fields_kernel), "y6", [pencil] * 5 + [(R, plan.NYC, 2 * plan.NXC)],
        [rest, height, vert], tables=[y_inv], work=[work(6)], cost=9.0, limit=20,
    )
    second, edges = lax.optimization_barrier((x_stage(second, (0,), ((0, 1), (0, 2))), edges))
    second = exchange(second, both)
    current = exchange(coarse, "row")
    surface_u, surface_v = call(bind(current_kernel), "currents", [(ny, nx)] * 2, [current])

    flow = pl.pallas_call(
        flow_kernel,
        grid=(levels,),
        out_shape=jax.ShapeDtypeStruct(velocity.shape, F32),
        in_specs=[smem, at(-1), at(0), at(1)]
        + edge_specs
        + [whole(x) for x in (surface_u, surface_v)],
        out_specs=at(0),
        compiler_params=pltpu.CompilerParams(vmem_limit_bytes=16 * MIB),
        cost_estimate=priced(19.0),
        name="flow",
    )(decay, velocity, velocity, velocity, *edges, surface_u, surface_v)

    last, vertical = call(
        bind(third_kernel), "y2", [spec(1), pencil], [second, height, vertical, third],
        tables=[y_inv, y_fwd], work=[work(2)],
    )
    last = exchange(x_stage(exchange(last, both), (0,), ((0, 1),)), both)
    (rates,) = call(
        bind(rates_kernel), "y3", [(R, 2 * N, W)], [last, vertical, slope, rate, energy],
        tables=[y_inv], work=[work(1)],
    )
    rates, flow = lax.optimization_barrier((exchange(rates, "row"), flow))
    tile = surface_height.shape
    height_rate, potential_rate, pressure, *sides = call(
        bind(tile_kernel), "tile", [tile, tile, (ny, nx)] + [(8, nx)] * 2 + [(8, ny)] * 2,
        [rates, surface_height],
    )
    sides = from_neighbours(*sides)
    pair = pl.BlockSpec((2, depth, ny, nx), lambda l: (0, l, 0, 0))
    velocity_next = pl.pallas_call(
        functools.partial(load_kernel, depth),
        grid=(levels // depth,),
        out_shape=jax.ShapeDtypeStruct(velocity.shape, F32),
        in_specs=[smem, pair] + [whole(x) for x in (pressure, *sides)],
        out_specs=pair,
        scratch_shapes=[pltpu.VMEM((ny, nx), F32)] * 2,
        input_output_aliases={1: 0},
        compiler_params=pltpu.CompilerParams(vmem_limit_bytes=16 * MIB),
        cost_estimate=priced(4.0),
        name="load",
    )(decay, flow, pressure, *sides)
    return height_rate, potential_rate, velocity_next


def solution(mesh):
    placed = (P("row", "col"), P("row", "col"), P(None, None, "row", "col"))
    return jax.shard_map(
        local,
        mesh=mesh,
        in_specs=placed,
        out_specs=placed,
        check_vma=False,
    )
```

time: 312 us -> 270 us (0.87)
  blocking collectives: 71.2 us -> 30.9 us
  other arithmetic: 33.2 us -> 11.1 us
  Pallas kernels: 81.4 us -> 59.6 us
  local copies, waits for them, and re-layouts: 17.7 us -> 34.6 us
  starting transfers between devices: 29.8 us -> 43 us
  waiting for transfers between devices: 72.2 us -> 84.8 us
    all_to_all x4 -> x2, blocking collectives: 71.2 us -> 30.9 us  [exchange(): return lax.all_to_all(x, axes, split_axis=0, concat_axis=0, tiled=True)]
    unnamed x10 -> x82, local copies, waits for them, and re-layouts: 7.6 us -> 34.5 us
    cos x4 -> x0, other arithmetic: 23.8 us -> none  [the longest x1 8.39 us: make_tables(): x_inv = parts(jnp.concatenate([jnp.cos(angle), jnp.sin(angle)], axis=1))]
    ppermute x8, waiting for transfers between devices: 6.5 us -> 29 us  [shift(): lax.ppermute(x, axis, [(i, (i + step) % peers) for i in range(peers)])]
    pallas_call x10 -> x15, Pallas kernels: 81.4 us -> 59.6 us  [the longest x12 36.9 us: call(): pl.pallas_call(kernel, out_shape=[jax.ShapeDtypeStruct(o, F32) for o in o...]
    all_to_all x4 -> x8, starting transfers between devices: 20.8 us -> 33.5 us  [exchange(): return lax.all_to_all(x, axes, split_axis=0, concat_axis=0, tiled=True)]
    all_to_all x4 -> x8, waiting for transfers between devices: 65.7 us -> 55.8 us  [exchange(): return lax.all_to_all(x, axes, split_axis=0, concat_axis=0, tiled=True)]
    slice x4 -> x0, local copies, waits for them, and re-layouts: 8.09 us -> none  [the longest x1 5.48 us: local(): velocity[:, :, :, -1]]
  transfers between devices with their start and end apart: 12 -> 16, of which waited for: 5 -> 9; matrix products, arithmetic and copies ran while one was open for 15% -> 4% of each run, Pallas kernels for 0% -> 14%
where the time goes in v2:
time: 270 us; the launch traced here: 265 us
  waiting for transfers between devices  84.8 us (31%)
  Pallas kernels  59.6 us (22%)
  starting transfers between devices  43 us (16%)
  local copies, waits for them, and re-layouts  34.6 us (13%)
  blocking collectives  30.9 us (11%)
  other arithmetic  11.1 us (4%)
    all_to_all x8, waiting for transfers between devices, exchange(): return lax.all_to_all(x, axes, split_axis=0, concat_axis=0, tiled=True)  55.8 us
    pallas_call x12, Pallas kernels, call(): pl.pallas_call(kernel, out_shape=[jax.ShapeDtypeStruct(o, F32) for o in o...  36.9 us
    unnamed x82, local copies, waits for them, and re-layouts  34.5 us
    all_to_all x8, starting transfers between devices, exchange(): return lax.all_to_all(x, axes, split_axis=0, concat_axis=0, tiled=True)  33.5 us
    all_to_all x2, blocking collectives, exchange(): return lax.all_to_all(x, axes, split_axis=0, concat_axis=0, tiled=True)  30.9 us
    ppermute x8, waiting for transfers between devices, shift(): lax.ppermute(x, axis, [(i, (i + step) % peers) for i in range(peers)])  29 us
    pallas_call x1, Pallas kernels, local(): pl.pallas_call(flow_kernel, grid=(levels,), out_shape=jax.ShapeDtypeStruc...  14.4 us
    ppermute x8, starting transfers between devices, shift(): lax.ppermute(x, axis, [(i, (i + step) % peers) for i in range(peers)])  9.51 us
  transfers between devices with their start and end apart: 16, of which 9 were waited for; matrix products, arithmetic and copies ran while one was open for 4% of the time, Pallas kernels for 14%

profile of v2, /device:TPU:3, one launch (start us, length us, event | category | flops | bytes accessed | tf_op | source)
XLA Modules:
  0.0 265.0 jit_solution(15473104502189160892)
XLA Ops:
  4.0 4.5 %all-to-all-start = ((f32[8,256,128]{2,1,0:T(8,128)}), f32[8,256,128]{2,1,0:T(8,128)S(1)}, u32[]{:S(2)}, u32[]{:S(2)}) async-start(f32[8,256,128]{2,1,0:T(8,128)} %pack.1), calls=%async_computation | async-start | bytes 2097152 | tf_op jit(solution)/shard_map/all_to_all | solution.py:563
  9.9 12.5 %all-to-all-done.in_ref = f32[8,256,128]{2,1,0:T(8,128)S(1)} async-done(((f32[8,256,128]{2,1,0:T(8,128)}), f32[8,256,128]{2,1,0:T(8,128)S(1)}, u32[]{:S(2)}, u32[]{:S(2)}) %all-to-all-start) | async-done | bytes 1048608 | tf_op jit(solution)/shard_map/all_to_all | solution.py:563
  25.0 5.3 %all-to-all-start.1 = ((f32[32,48,128]{2,1,0:T(8,128)}), f32[32,48,128]{2,1,0:T(8,128)S(1)}, u32[]{:S(2)}, u32[]{:S(2)}) async-start(f32[32,48,128]{2,1,0:T(8,128)} %copy-done.15), calls=%async_computation.1 | async-start | bytes 1572864 | tf_op jit(solution)/shard_map/all_to_all | solution.py:563
  30.5 2.1 fusion.6
  34.6 2.1 fusion
  36.7 14.3 %all-to-all-done.1.in_ref = f32[32,48,128]{2,1,0:T(8,128)S(1)} async-done(((f32[32,48,128]{2,1,0:T(8,128)}), f32[32,48,128]{2,1,0:T(8,128)S(1)}, u32[]{:S(2)}, u32[]{:S(2)}) %all-to-all-start.1) | async-done | bytes 786464 | tf_op jit(solution)/shard_map/all_to_all | solution.py:563
  52.6 2.9 %x1.2 = f32[32,24,128]{2,1,0:T(8,128)S(1)} custom-call(s32[2]{0:T(128)S(1)} %pad_add_fusion.place_ref, f32[32,48,128]{2,1,0:T(8,128)S(1)} %all-to-all-done.1.in_ref, bf16[4,512,512]{2,1,0:T(8,128)(2,1)S(1)} %copy-done.6, bf16[4,512,512]{2,1,0:T(8,128)(2,1)S(1)} %get-tuple-element.115.fl), custom_call_target="tpu_custom_call" | custom-call | flops 1200000000 | bytes 4000000 | tf_op jit(solution)/shard_map/x1/pallas_call | solution.py:544
  56.3 3.4 %all-to-all-start.2 = ((f32[32,24,128]{2,1,0:T(8,128)}), f32[32,24,128]{2,1,0:T(8,128)}, u32[]{:S(2)}, u32[]{:S(2)}) async-start(f32[32,24,128]{2,1,0:T(8,128)} %copy-done.14), calls=%async_computation.2 | async-start | bytes 786432 | tf_op jit(solution)/shard_map/all_to_all | solution.py:563
  63.2 8.9 %all-to-all-done.2.buf_ref = f32[32,24,128]{2,1,0:T(8,128)} async-done(((f32[32,24,128]{2,1,0:T(8,128)}), f32[32,24,128]{2,1,0:T(8,128)}, u32[]{:S(2)}, u32[]{:S(2)}) %all-to-all-start.2) | async-done | bytes 393248 | tf_op jit(solution)/shard_map/all_to_all | solution.py:563
  73.5 3.3 %y1.1 = (f32[32,24,128]{2,1,0:T(8,128)S(1)}, f32[8,128,128]{2,1,0:T(8,128)S(1)}) custom-call(f32[32,24,128]{2,1,0:T(8,128)} %all-to-all-done.2.buf_ref, f32[8,128,128]{2,1,0:T(8,128)S(1)} %get-tuple-element.76.height_ref, bf16[8,512,192]{2,1,0:T(8,128)(2,1)S(1)} %pad_maximum_fusion.2.yi, bf16[8,192,512]{2,1,0:T(8,128)(2,1)S(1)} %copy-done.11), custom_call_target="tpu_custom_call" | custom-call | flops 1200000000 | bytes 4000000 | tf_op jit(solution)/shard_map/y1/pallas_call | solution.py:544
  78.3 3.4 %all-to-all-start.3 = ((f32[32,24,128]{2,1,0:T(8,128)}), f32[32,24,128]{2,1,0:T(8,128)}, u32[]{:S(2)}, u32[]{:S(2)}) async-start(f32[32,24,128]{2,1,0:T(8,128)} %copy-done.29), calls=%async_computation.3 | async-start | bytes 786432 | tf_op jit(solution)/shard_map/all_to_all | solution.py:563
  84.9 5.8 %x6.1 = f32[32,144,128]{2,1,0:T(8,128)S(1)} custom-call(s32[2]{0:T(128)S(1)} %pad_add_fusion.place_ref, f32[32,48,128]{2,1,0:T(8,128)S(1)} %all-to-all-done.1.in_ref, bf16[4,512,512]{2,1,0:T(8,128)(2,1)S(1)} %copy-done.7, bf16[4,512,512]{2,1,0:T(8,128)(2,1)S(1)} %copy-done.3), custom_call_target="tpu_custom_call" | custom-call | flops 2700000000 | bytes 9000000 | tf_op jit(solution)/shard_map/x6/pallas_call | solution.py:544
  94.1 3.9 %all-to-all-start.5 = ((f32[32,144,128]{2,1,0:T(8,128)}), f32[32,144,128]{2,1,0:T(8,128)}, u32[]{:S(2)}, u32[]{:S(2)}) async-start(f32[32,144,128]{2,1,0:T(8,128)} %copy-done.13), calls=%async_computation.5 | async-start | bytes 4718592 | tf_op jit(solution)/shard_map/all_to_all | solution.py:563
  98.0 2.8 %copy-done = f32[3,16,128,256]{3,2,1,0:T(8,128)S(1)} copy-done((f32[3,16,128,256]{3,2,1,0:T(8,128)S(1)}, f32[3,16,128,256]{3,2,1,0:T(8,128)}, u32[]{:S(2)}) %copy-start) | copy-done | bytes 6291480
  100.8 3.2 %edges.1 = (f32[16,8,256]{2,1,0:T(8,128)S(1)}, f32[16,8,256]{2,1,0:T(8,128)S(1)}, f32[16,8,128]{2,1,0:T(8,128)S(1)}, f32[16,8,128]{2,1,0:T(8,128)S(1)}) custom-call(f32[3,16,128,256]{3,2,1,0:T(8,128)S(1)} %copy-done), custom_call_target="tpu_custom_call" | custom-call | flops 1500000000 | bytes 5000000 | tf_op jit(solution)/shard_map/edges/pallas_call | solution.py:604
  106.6 2.1 collective-permute-start.3
  108.7 3.9 %x2.1 = f32[32,48,128]{2,1,0:T(8,128)S(1)} custom-call(s32[2]{0:T(128)S(1)} %pad_add_fusion.place_ref, f32[32,24,128]{2,1,0:T(8,128)} %all-to-all-done.3.in_ref, bf16[4,512,512]{2,1,0:T(8,128)(2,1)S(1)} %copy-done.8, bf16[4,512,512]{2,1,0:T(8,128)(2,1)S(1)} %copy-done.4), custom_call_target="tpu_custom_call" | custom-call | flops 1500000000 | bytes 5000000 | tf_op jit(solution)/shard_map/x2/pallas_call | solution.py:544
  113.5 27.9 %collective-permute-done.2.west_ref = f32[16,8,128]{2,1,0:T(8,128)S(1)} collective-permute-done((f32[16,8,128]{2,1,0:T(8,128)S(1)}, f32[16,8,128]{2,1,0:T(8,128)S(1)}, u32[]{:S(2)}, u32[]{:S(2)}) %collective-permute-start.2) | collective-permute-done | bytes 65568 | tf_op jit(solution)/shard_map/ppermute | solution.py:568
  143.3 10.6 %all-to-all-done.5.buf_ref = f32[32,144,128]{2,1,0:T(8,128)} async-done(((f32[32,144,128]{2,1,0:T(8,128)}), f32[32,144,128]{2,1,0:T(8,128)}, u32[]{:S(2)}, u32[]{:S(2)}) %all-to-all-start.5) | async-done | bytes 2359328 | tf_op jit(solution)/shard_map/all_to_all | solution.py:563
  153.9 5.8 %all-to-all-start.4 = ((f32[32,48,128]{2,1,0:T(8,128)}), f32[32,48,128]{2,1,0:T(8,128)S(1)}, u32[]{:S(2)}, u32[]{:S(2)}) async-start(f32[32,48,128]{2,1,0:T(8,128)} %copy-done.16), calls=%async_computation.4 | async-start | bytes 1572864 | tf_op jit(solution)/shard_map/all_to_all | solution.py:563
  160.7 8.0 %y6.1 = (f32[8,128,128]{2,1,0:T(8,128)S(1)}, f32[8,128,128]{2,1,0:T(8,128)S(1)}, f32[8,128,128]{2,1,0:T(8,128)S(1)}, f32[8,128,128]{2,1,0:T(8,128)S(1)}, f32[8,1...) custom-call(f32[32,144,128]{2,1,0:T(8,128)} %all-to-all-done.5.buf_ref, f32[8,128,128]{2,1,0:T(8,128)S(1)} %get-tuple-element.76.height_ref, ...), custom_call_target="tpu_custom_call" | custom-call | flops 2700000000 | bytes 9000000 | tf_op jit(solution)/shard_map/y6/pallas_call | solution.py:544
  172.8 7.5 %all-to-all-done.4.buf_ref = f32[32,48,128]{2,1,0:T(8,128)S(1)} async-done(((f32[32,48,128]{2,1,0:T(8,128)}), f32[32,48,128]{2,1,0:T(8,128)S(1)}, u32[]{:S(2)}, u32[]{:S(2)}) %all-to-all-start.4) | async-done | bytes 786464 | tf_op jit(solution)/shard_map/all_to_all | solution.py:563
  183.8 2.6 y2.1
  186.4 15.5 %all_to_all.50.in_ref = f32[32,24,128]{2,1,0:T(8,128)S(1)} all-to-all(f32[32,24,128]{2,1,0:T(8,128)S(1)} %get-tuple-element.94), channel_id=1, replica_groups=mesh['row'=8,'col'=4] {'row','col'}, dimensions={0} | all-to-all | bytes 786432 | tf_op jit(solution)/shard_map/all_to_all | solution.py:563
  201.9 2.9 %x1.3 = f32[32,24,128]{2,1,0:T(8,128)S(1)} custom-call(s32[2]{0:T(128)S(1)} %pad_add_fusion.place_ref, f32[32,24,128]{2,1,0:T(8,128)S(1)} %all_to_all.50.in_ref, bf16[4,512,512]{2,1,0:T(8,128)(2,1)S(1)} %copy-done.9, bf16[4,512,512]{2,1,0:T(8,128)(2,1)S(1)} %copy-done.5), custom_call_target="tpu_custom_call" | custom-call | flops 1200000000 | bytes 4000000 | tf_op jit(solution)/shard_map/x1/pallas_call | solution.py:544
  204.8 15.5 %all_to_all.51.buf_ref = f32[32,24,128]{2,1,0:T(8,128)S(1)} all-to-all(f32[32,24,128]{2,1,0:T(8,128)S(1)} %x1.3), channel_id=1, replica_groups=mesh['row'=8,'col'=4] {'row','col'}, dimensions={0} | all-to-all | bytes 786432 | tf_op jit(solution)/shard_map/all_to_all | solution.py:563
  220.3 3.4 %all-to-all-start.9 = ((f32[8,64,128]{2,1,0:T(8,128)}), f32[8,64,128]{2,1,0:T(8,128)S(1)}, u32[]{:S(2)}, u32[]{:S(2)}) async-start(f32[8,64,128]{2,1,0:T(8,128)} %get-tuple-element.103), calls=%async_computation.9 | async-start | bytes 524288 | tf_op jit(solution)/shard_map/all_to_all | solution.py:563
  227.8 2.4 y3.1
  230.3 3.9 %all-to-all-start.8 = ((f32[8,256,128]{2,1,0:T(8,128)}), f32[8,256,128]{2,1,0:T(8,128)S(1)}, u32[]{:S(2)}, u32[]{:S(2)}) async-start(f32[8,256,128]{2,1,0:T(8,128)} %y3.1), calls=%async_computation.8 | async-start | bytes 2097152 | tf_op jit(solution)/shard_map/all_to_all | solution.py:563
  235.2 2.8 %copy-done.1 = f32[3,16,128,256]{3,2,1,0:T(8,128)S(1)} copy-done((f32[3,16,128,256]{3,2,1,0:T(8,128)S(1)}, f32[3,16,128,256]{3,2,1,0:T(8,128)}, u32[]{:S(2)}) %copy-start.1) | copy-done | bytes 6291480
  238.0 14.4 %flow.1.flow_ref = f32[3,16,128,256]{3,2,1,0:T(8,128)} custom-call(f32[16,2]{1,0:T(8,128)S(1)} %copy.7.decay_ref, f32[3,16,128,256]{3,2,1,0:T(8,128)S(1)} %copy-done.1, f32[3,16,128,256]{3,2,1,0:T(8,128)S(1)} %copy-done.1, f32[3,16,128,256]{3,2,1,0:T(8,128)S(1)} %copy-done.1, f32[16,8,256]{2,1,0:T(8,128)S(1)} %collective-permute-done.south_ref, ...), custom_call_target="tpu_custom_call" | custom-call | flops 5699999744 | bytes 19000000 | tf_op jit(solution)/shard_map/flow/pallas_call | solution.py:658
  259.9 5.1 %load.1 = f32[3,16,128,256]{3,2,1,0:T(8,128)} custom-call(f32[16,2]{1,0:T(8,128)S(1)} %copy.7.decay_ref, f32[3,16,128,256]{3,2,1,0:T(8,128)} %flow.1.flow_ref, f32[128,256]{1,0:T(8,128)S(1)} %get-tuple-element.110.pressure_ref, f32[8,256]{1,0:T(8,128)S(1)} %collective-permute-done.4.south_ref, ...), custom_call_target="tpu_custom_call", output_to_operand_aliasing={{}: (1, {})} | custom-call | flops 1200000000 | bytes 4000000 | tf_op jit(solution)/shard_map/load/pallas_call | solution.py:688
  (129 shorter events, 51.5 us)
Async XLA Ops:
  4.0 18.4 %all-to-all-start = ((f32[8,256,128]{2,1,0:T(8,128)}), f32[8,256,128]{2,1,0:T(8,128)S(1)}, u32[]{:S(2)}, u32[]{:S(2)}) async-start(f32[8,256,128]{2,1,0:T(8,128)} %pack.1), calls=%async_computation | async-start | bytes 2097152 | tf_op jit(solution)/shard_map/all_to_all | solution.py:563
  9.9 14.3 %copy-start.10 = (bf16[8,192,512]{2,1,0:T(8,128)(2,1)}, bf16[8,192,512]{2,1,0:T(8,128)(2,1)S(1)}, u32[]{:S(2)}) copy-start(bf16[8,192,512]{2,1,0:T(8,128)(2,1)S(1)} %pad_maximum_fusion.4.yf) | copy-start | bytes 4718596
  25.0 26.0 %all-to-all-start.1 = ((f32[32,48,128]{2,1,0:T(8,128)}), f32[32,48,128]{2,1,0:T(8,128)S(1)}, u32[]{:S(2)}, u32[]{:S(2)}) async-start(f32[32,48,128]{2,1,0:T(8,128)} %copy-done.15), calls=%async_computation.1 | async-start | bytes 1572864 | tf_op jit(solution)/shard_map/all_to_all | solution.py:563
  36.7 18.8 %copy-start.2 = (bf16[4,512,512]{2,1,0:T(8,128)(2,1)}, bf16[4,512,512]{2,1,0:T(8,128)(2,1)S(1)}, u32[]{:S(2)}) copy-start(bf16[4,512,512]{2,1,0:T(8,128)(2,1)S(1)} %get-tuple-element.115.fl) | copy-start | bytes 6291460
  51.0 1.6 copy-start.6
  56.3 15.8 %all-to-all-start.2 = ((f32[32,24,128]{2,1,0:T(8,128)}), f32[32,24,128]{2,1,0:T(8,128)}, u32[]{:S(2)}, u32[]{:S(2)}) async-start(f32[32,24,128]{2,1,0:T(8,128)} %copy-done.14), calls=%async_computation.2 | async-start | bytes 786432 | tf_op jit(solution)/shard_map/all_to_all | solution.py:563
  72.1 1.4 copy-start.11
  78.3 15.8 %all-to-all-start.3 = ((f32[32,24,128]{2,1,0:T(8,128)}), f32[32,24,128]{2,1,0:T(8,128)}, u32[]{:S(2)}, u32[]{:S(2)}) async-start(f32[32,24,128]{2,1,0:T(8,128)} %copy-done.29), calls=%async_computation.3 | async-start | bytes 786432 | tf_op jit(solution)/shard_map/all_to_all | solution.py:563
  81.7 1.6 copy-start.3
  83.3 1.6 copy-start.7
  90.7 1.4 copy-start.13
  94.1 59.8 %all-to-all-start.5 = ((f32[32,144,128]{2,1,0:T(8,128)}), f32[32,144,128]{2,1,0:T(8,128)}, u32[]{:S(2)}, u32[]{:S(2)}) async-start(f32[32,144,128]{2,1,0:T(8,128)} %copy-done.13), calls=%async_computation.5 | async-start | bytes 4718592 | tf_op jit(solution)/shard_map/all_to_all | solution.py:563
  98.0 2.8 %copy-start = (f32[3,16,128,256]{3,2,1,0:T(8,128)S(1)}, f32[3,16,128,256]{3,2,1,0:T(8,128)}, u32[]{:S(2)}) copy-start(f32[3,16,128,256]{3,2,1,0:T(8,128)} %next_ref.1) | copy-start | bytes 18874372
  100.8 8.0 %copy-start.4 = (bf16[4,512,512]{2,1,0:T(8,128)(2,1)S(1)}, bf16[4,512,512]{2,1,0:T(8,128)(2,1)}, u32[]{:S(2)}) copy-start(bf16[4,512,512]{2,1,0:T(8,128)(2,1)} %copy-done.2) | copy-start | bytes 6291460
  100.8 8.0 %copy-start.8 = (bf16[4,512,512]{2,1,0:T(8,128)(2,1)S(1)}, bf16[4,512,512]{2,1,0:T(8,128)(2,1)}, u32[]{:S(2)}) copy-start(bf16[4,512,512]{2,1,0:T(8,128)(2,1)} %get-tuple-element.116.fh) | copy-start | bytes 6291460
  103.9 38.7 %collective-permute-start = (f32[16,8,256]{2,1,0:T(8,128)S(1)}, f32[16,8,256]{2,1,0:T(8,128)S(1)}, u32[]{:S(2)}, u32[]{:S(2)}) collective-permute-start(f32[16,8,256]{2,1,0:T(8,128)S(1)} %get-tuple-element.86), channel_id=1, source_target_pairs={{0,4},{4,8},{8,12},{12,16},{16,20},{20,24},{24,28},{28,0},{1,5},{5... | collective-permute-start | bytes 393224 | tf_op jit(solution)/shard_map/ppermute | solution.py:568
  105.5 37.2 %collective-permute-start.1 = (f32[16,8,256]{2,1,0:T(8,128)S(1)}, f32[16,8,256]{2,1,0:T(8,128)S(1)}, u32[]{:S(2)}, u32[]{:S(2)}) collective-permute-start(f32[16,8,256]{2,1,0:T(8,128)S(1)} %get-tuple-element.87), channel_id=1, source_target_pairs={{0,28},{4,0},{8,4},{12,8},{16,12},{20,16},{24,20},{28,24},{1,29},{... | collective-permute-start | bytes 393224 | tf_op jit(solution)/shard_map/ppermute | solution.py:568
  105.5 36.0 %collective-permute-start.2 = (f32[16,8,128]{2,1,0:T(8,128)S(1)}, f32[16,8,128]{2,1,0:T(8,128)S(1)}, u32[]{:S(2)}, u32[]{:S(2)}) collective-permute-start(f32[16,8,128]{2,1,0:T(8,128)S(1)} %get-tuple-element.88), channel_id=1, source_target_pairs={{0,1},{1,2},{2,3},{3,0},{4,5},{5,6},{6,7},{7,4},{8,9},{9,10},{10,1... | collective-permute-start | bytes 196616 | tf_op jit(solution)/shard_map/ppermute | solution.py:568
  106.6 35.4 %collective-permute-start.3 = (f32[16,8,128]{2,1,0:T(8,128)S(1)}, f32[16,8,128]{2,1,0:T(8,128)S(1)}, u32[]{:S(2)}, u32[]{:S(2)}) collective-permute-start(f32[16,8,128]{2,1,0:T(8,128)S(1)} %get-tuple-element.89), channel_id=1, source_target_pairs={{0,3},{1,0},{2,1},{3,2},{4,7},{5,4},{6,5},{7,6},{8,11},{9,8},{10,9... | collective-permute-start | bytes 196616 | tf_op jit(solution)/shard_map/ppermute | solution.py:568
  153.9 26.4 %all-to-all-start.4 = ((f32[32,48,128]{2,1,0:T(8,128)}), f32[32,48,128]{2,1,0:T(8,128)S(1)}, u32[]{:S(2)}, u32[]{:S(2)}) async-start(f32[32,48,128]{2,1,0:T(8,128)} %copy-done.16), calls=%async_computation.4 | async-start | bytes 1572864 | tf_op jit(solution)/shard_map/all_to_all | solution.py:563
  180.3 1.4 copy-start.12
  183.8 18.1 %copy-start.5 = (bf16[4,512,512]{2,1,0:T(8,128)(2,1)S(1)}, bf16[4,512,512]{2,1,0:T(8,128)(2,1)}, u32[]{:S(2)}) copy-start(bf16[4,512,512]{2,1,0:T(8,128)(2,1)} %copy-done.2) | copy-start | bytes 6291460
  183.8 18.1 %copy-start.9 = (bf16[4,512,512]{2,1,0:T(8,128)(2,1)S(1)}, bf16[4,512,512]{2,1,0:T(8,128)(2,1)}, u32[]{:S(2)}) copy-start(bf16[4,512,512]{2,1,0:T(8,128)(2,1)} %get-tuple-element.116.fh) | copy-start | bytes 6291460
  186.4 18.4 %copy-start.27 = (f32[8,128,128]{2,1,0:T(8,128)}, f32[8,128,128]{2,1,0:T(8,128)S(1)}, u32[]{:S(2)}) copy-start(f32[8,128,128]{2,1,0:T(8,128)S(1)} %get-tuple-element.95.vertical_in) | copy-start | bytes 1572868
  220.3 10.0 %all-to-all-start.9 = ((f32[8,64,128]{2,1,0:T(8,128)}), f32[8,64,128]{2,1,0:T(8,128)S(1)}, u32[]{:S(2)}, u32[]{:S(2)}) async-start(f32[8,64,128]{2,1,0:T(8,128)} %get-tuple-element.103), calls=%async_computation.9 | async-start | bytes 524288 | tf_op jit(solution)/shard_map/all_to_all | solution.py:563
  230.3 22.2 %all-to-all-start.8 = ((f32[8,256,128]{2,1,0:T(8,128)}), f32[8,256,128]{2,1,0:T(8,128)S(1)}, u32[]{:S(2)}, u32[]{:S(2)}) async-start(f32[8,256,128]{2,1,0:T(8,128)} %y3.1), calls=%async_computation.8 | async-start | bytes 2097152 | tf_op jit(solution)/shard_map/all_to_all | solution.py:563
  235.2 2.8 %copy-start.1 = (f32[3,16,128,256]{3,2,1,0:T(8,128)S(1)}, f32[3,16,128,256]{3,2,1,0:T(8,128)}, u32[]{:S(2)}) copy-start(f32[3,16,128,256]{3,2,1,0:T(8,128)} %next_ref.1) | copy-start | bytes 18874372
  238.0 14.4 %copy-start.38 = (f32[256,512]{1,0:T(8,128)S(1)}, f32[256,512]{1,0:T(8,128)}, u32[]{:S(2)}) copy-start(f32[256,512]{1,0:T(8,128)} %height_ref.3) | copy-start | bytes 1572868
  254.1 5.8 %collective-permute-start.4 = (f32[8,256]{1,0:T(8,128)S(1)}, f32[8,256]{1,0:T(8,128)S(1)}, u32[]{:S(2)}, u32[]{:S(2)}) collective-permute-start(f32[8,256]{1,0:T(8,128)S(1)} %get-tuple-element.111), channel_id=1, source_target_pairs={{0,4},{4,8},{8,12},{12,16},{16,20},{20,24},{24,28},{28,0},{1,5},{5... | collective-permute-start | bytes 24584 | tf_op jit(solution)/shard_map/ppermute | solution.py:568
  255.6 4.3 %collective-permute-start.5 = (f32[8,256]{1,0:T(8,128)S(1)}, f32[8,256]{1,0:T(8,128)S(1)}, u32[]{:S(2)}, u32[]{:S(2)}) collective-permute-start(f32[8,256]{1,0:T(8,128)S(1)} %get-tuple-element.112), channel_id=1, source_target_pairs={{0,28},{4,0},{8,4},{12,8},{16,12},{20,16},{24,20},{28,24},{1,29},{... | collective-permute-start | bytes 24584 | tf_op jit(solution)/shard_map/ppermute | solution.py:568
  255.6 4.3 %collective-permute-start.6 = (f32[8,128]{1,0:T(8,128)S(1)}, f32[8,128]{1,0:T(8,128)S(1)}, u32[]{:S(2)}, u32[]{:S(2)}) collective-permute-start(f32[8,128]{1,0:T(8,128)S(1)} %get-tuple-element.113), channel_id=1, source_target_pairs={{0,1},{1,2},{2,3},{3,0},{4,5},{5,6},{6,7},{7,4},{8,9},{9,10},{10,1... | collective-permute-start | bytes 12296 | tf_op jit(solution)/shard_map/ppermute | solution.py:568
  257.5 2.5 collective-permute-start.7
  (25 other events, 22.1 us)

commit v3 on v2

--- a/solution.py
+++ b/solution.py
@@ -447,7 +447,7 @@
     top_u, top_v = u_ref[...], v_ref[...]
     is_top = level == 0
 
-    def derivs(q, top):
+    def differences(q, top):
         mid = cur_ref[q, 0]
         east, west, north, south = around(
             mid,
@@ -458,24 +458,28 @@
         )
         above = jnp.where(is_top, top, prev_ref[q, 0])
         below = next_ref[q, 0]
-        lap = (east + west) + (north + south) + (above + below) - 6.0 * mid
-        return mid, 0.5 * (east - west), 0.5 * (north - south), 0.5 * (above - below), lap
-
-    u, u_dx, u_dy, u_dz, u_lap = derivs(0, top_u)
-    v, v_dx, v_dy, v_dz, v_lap = derivs(1, top_v)
-    w, w_dx, w_dy, w_dz, w_lap = derivs(2, jnp.zeros_like(top_u))
-    drift_u = top_u * decay_ref[level, 0]
-    drift_v = top_v * decay_ref[level, 0]
+        total = (east + west) + (north + south) + (above + below)
+        return mid, east - west, north - south, above - below, total
+
+    u, u_dx, u_dy, u_dz, u_sum = differences(0, top_u)
+    v, v_dx, v_dy, v_dz, v_sum = differences(1, top_v)
+    w, w_dx, w_dy, w_dz, w_sum = differences(2, 0.0)
+    half = 0.5 * FLOW_STEP
+    fall = half * decay_ref[level, 0]
+    drift_u, drift_v = top_u * fall, top_v * fall
     vort_x = w_dy - v_dz
     vort_y = u_dz - w_dx
     vort_z = v_dx - u_dy
-
-    def advance(mid, dx, dy, dz, lap, force):
-        return mid + FLOW_STEP * (VISCOSITY * lap + force - (u * dx + v * dy + w * dz))
-
-    out_ref[0, 0] = advance(u, u_dx, u_dy, u_dz, u_lap, drift_v * vort_z)
-    out_ref[1, 0] = advance(v, v_dx, v_dy, v_dz, v_lap, -drift_u * vort_z)
-    out_ref[2, 0] = advance(w, w_dx, w_dy, w_dz, w_lap, drift_u * vort_y - drift_v * vort_x)
+    spread_by = FLOW_STEP * VISCOSITY
+    half_u, half_v, half_w = half * u, half * v, half * w
+
+    def advance(mid, dx, dy, dz, total, force):
+        carried = half_u * dx + half_v * dy + half_w * dz
+        return (1.0 - 6.0 * spread_by) * mid + spread_by * total + (force - carried)
+
+    out_ref[0, 0] = advance(u, u_dx, u_dy, u_dz, u_sum, drift_v * vort_z)
+    out_ref[1, 0] = advance(v, v_dx, v_dy, v_dz, v_sum, -drift_u * vort_z)
+    out_ref[2, 0] = advance(w, w_dx, w_dy, w_dz, w_sum, drift_u * vort_y - drift_v * vort_x)
 
 
 def load_kernel(
@@ -529,8 +533,7 @@
     coarse = turns(R * ints(plan.KY, 0, 2), ints(plan.NYL, 0, 1), NY)
     fine = turns(ints(R, 1, 2), ints(plan.NYL, 0, 1), NY)
     y_fwd = jnp.concatenate(parts(table(coarse, fine, 2)), axis=1)
-    coarse = turns(R * ints(plan.KY, 0, 1), ints(plan.NYL, 0, 2), NY)
-    fine = turns(ints(R, 1, 2), ints(plan.NYL, 0, 2), NY)
+    coarse, fine = [tuple(jnp.swapaxes(x, 1, 2) for x in t) for t in (coarse, fine)]
     y_inv = jnp.concatenate(parts(table(coarse, fine, 2)), axis=1)
     coarse = turns(C * ints(plan.J, 0, 1), ints(plan.NXL, 0, 2), NX)
     fine = turns(ints(C, 1, 2), ints(plan.NXL, 0, 2), NX)
@@ -592,7 +595,7 @@
     packed = exchange(packed, "row")
 
     levels, ny, nx = velocity.shape[1:]
-    depth = 4 if levels % 4 == 0 else 1
+    depth = 2 if levels % 2 == 0 else 1
     block = (3, 1, ny, nx)
     at = lambda step: pl.BlockSpec(
         block, lambda l: (0, jnp.clip(l + step, 0, levels - 1), 0, 0)

time: 270 us -> 272 us (level)
    unnamed x82 -> x86, local copies, waits for them, and re-layouts: 34.5 us -> 34.5 us
  transfers between devices with their start and end apart: 16 -> 16, of which waited for: 9 -> 9; matrix products, arithmetic and copies ran while one was open for 4% -> 3% of each run, Pallas kernels for 14% -> 14%
where the time goes in v3:
time: 272 us; the launch traced here: 267 us
  waiting for transfers between devices  86.7 us (32%)
  Pallas kernels  61.5 us (23%)
  starting transfers between devices  43 us (16%)
  local copies, waits for them, and re-layouts  34.8 us (13%)
  blocking collectives  30.9 us (11%)
  other arithmetic  8.92 us (3%)
    all_to_all x8, waiting for transfers between devices, exchange(): return lax.all_to_all(x, axes, split_axis=0, concat_axis=0, tiled=True)  57.7 us
    pallas_call x12, Pallas kernels, call(): pl.pallas_call(kernel, out_shape=[jax.ShapeDtypeStruct(o, F32) for o in o...  36.9 us
    unnamed x86, local copies, waits for them, and re-layouts  34.5 us
    all_to_all x8, starting transfers between devices, exchange(): return lax.all_to_all(x, axes, split_axis=0, concat_axis=0, tiled=True)  33.5 us
    all_to_all x2, blocking collectives, exchange(): return lax.all_to_all(x, axes, split_axis=0, concat_axis=0, tiled=True)  30.9 us
    ppermute x8, waiting for transfers between devices, shift(): lax.ppermute(x, axis, [(i, (i + step) % peers) for i in range(peers)])  29 us
    pallas_call x1, Pallas kernels, local(): pl.pallas_call(flow_kernel, grid=(levels,), out_shape=jax.ShapeDtypeStruc...  14.5 us
    ppermute x8, starting transfers between devices, shift(): lax.ppermute(x, axis, [(i, (i + step) % peers) for i in range(peers)])  9.51 us
  transfers between devices with their start and end apart: 16, of which 9 were waited for; matrix products, arithmetic and copies ran while one was open for 3% of the time, Pallas kernels for 14%

profile of v3, /device:TPU:3, one launch (start us, length us, event | category | flops | bytes accessed | tf_op | source)
XLA Modules:
  0.0 267.0 jit_solution(11353711481642980992)
XLA Ops:
  4.0 4.5 %all-to-all-start = ((f32[8,256,128]{2,1,0:T(8,128)}), f32[8,256,128]{2,1,0:T(8,128)S(1)}, u32[]{:S(2)}, u32[]{:S(2)}) async-start(f32[8,256,128]{2,1,0:T(8,128)} %pack.1), calls=%async_computation | async-start | bytes 2097152 | tf_op jit(solution)/shard_map/all_to_all | solution.py:566
  10.2 12.2 %all-to-all-done.in_ref = f32[8,256,128]{2,1,0:T(8,128)S(1)} async-done(((f32[8,256,128]{2,1,0:T(8,128)}), f32[8,256,128]{2,1,0:T(8,128)S(1)}, u32[]{:S(2)}, u32[]{:S(2)}) %all-to-all-start) | async-done | bytes 1048608 | tf_op jit(solution)/shard_map/all_to_all | solution.py:566
  25.0 5.3 %all-to-all-start.1 = ((f32[32,48,128]{2,1,0:T(8,128)}), f32[32,48,128]{2,1,0:T(8,128)S(1)}, u32[]{:S(2)}, u32[]{:S(2)}) async-start(f32[32,48,128]{2,1,0:T(8,128)} %copy-done.15), calls=%async_computation.1 | async-start | bytes 1572864 | tf_op jit(solution)/shard_map/all_to_all | solution.py:566
  30.6 2.1 fusion.6
  33.4 2.1 fusion
  35.4 15.6 %all-to-all-done.1.in_ref = f32[32,48,128]{2,1,0:T(8,128)S(1)} async-done(((f32[32,48,128]{2,1,0:T(8,128)}), f32[32,48,128]{2,1,0:T(8,128)S(1)}, u32[]{:S(2)}, u32[]{:S(2)}) %all-to-all-start.1) | async-done | bytes 786464 | tf_op jit(solution)/shard_map/all_to_all | solution.py:566
  52.6 2.9 %x1.2 = f32[32,24,128]{2,1,0:T(8,128)S(1)} custom-call(s32[2]{0:T(128)S(1)} %pad_add_fusion.place_ref, f32[32,48,128]{2,1,0:T(8,128)S(1)} %all-to-all-done.1.in_ref, bf16[4,512,512]{2,1,0:T(8,128)(2,1)S(1)} %copy-done.6, bf16[4,512,512]{2,1,0:T(8,128)(2,1)S(1)} %get-tuple-element.99.fl), custom_call_target="tpu_custom_call" | custom-call | flops 1200000000 | bytes 4000000 | tf_op jit(solution)/shard_map/x1/pallas_call | solution.py:547
  56.3 3.4 %all-to-all-start.2 = ((f32[32,24,128]{2,1,0:T(8,128)}), f32[32,24,128]{2,1,0:T(8,128)}, u32[]{:S(2)}, u32[]{:S(2)}) async-start(f32[32,24,128]{2,1,0:T(8,128)} %copy-done.14), calls=%async_computation.2 | async-start | bytes 786432 | tf_op jit(solution)/shard_map/all_to_all | solution.py:566
  62.2 9.9 %all-to-all-done.2.buf_ref = f32[32,24,128]{2,1,0:T(8,128)} async-done(((f32[32,24,128]{2,1,0:T(8,128)}), f32[32,24,128]{2,1,0:T(8,128)}, u32[]{:S(2)}, u32[]{:S(2)}) %all-to-all-start.2) | async-done | bytes 393248 | tf_op jit(solution)/shard_map/all_to_all | solution.py:566
  73.5 3.3 %y1.1 = (f32[32,24,128]{2,1,0:T(8,128)S(1)}, f32[8,128,128]{2,1,0:T(8,128)S(1)}) custom-call(f32[32,24,128]{2,1,0:T(8,128)} %all-to-all-done.2.buf_ref, f32[8,128,128]{2,1,0:T(8,128)S(1)} %get-tuple-element.68.height_ref, bf16[8,512,192]{2,1,0:T(8,128)(2,1)S(1)} %pad_maximum_fusion.2.yi, bf16[8,192,512]{2,1,0:T(8,128)(2,1)S(1)} %copy-done.11), custom_call_target="tpu_custom_call" | custom-call | flops 1200000000 | bytes 4000000 | tf_op jit(solution)/shard_map/y1/pallas_call | solution.py:547
  78.3 3.4 %all-to-all-start.3 = ((f32[32,24,128]{2,1,0:T(8,128)}), f32[32,24,128]{2,1,0:T(8,128)}, u32[]{:S(2)}, u32[]{:S(2)}) async-start(f32[32,24,128]{2,1,0:T(8,128)} %copy-done.29), calls=%async_computation.3 | async-start | bytes 786432 | tf_op jit(solution)/shard_map/all_to_all | solution.py:566
  84.9 5.8 %x6.1 = f32[32,144,128]{2,1,0:T(8,128)S(1)} custom-call(s32[2]{0:T(128)S(1)} %pad_add_fusion.place_ref, f32[32,48,128]{2,1,0:T(8,128)S(1)} %all-to-all-done.1.in_ref, bf16[4,512,512]{2,1,0:T(8,128)(2,1)S(1)} %copy-done.7, bf16[4,512,512]{2,1,0:T(8,128)(2,1)S(1)} %copy-done.3), custom_call_target="tpu_custom_call" | custom-call | flops 2700000000 | bytes 9000000 | tf_op jit(solution)/shard_map/x6/pallas_call | solution.py:547
  94.1 3.9 %all-to-all-start.5 = ((f32[32,144,128]{2,1,0:T(8,128)}), f32[32,144,128]{2,1,0:T(8,128)}, u32[]{:S(2)}, u32[]{:S(2)}) async-start(f32[32,144,128]{2,1,0:T(8,128)} %copy-done.13), calls=%async_computation.5 | async-start | bytes 4718592 | tf_op jit(solution)/shard_map/all_to_all | solution.py:566
  98.0 2.8 %copy-done = f32[3,16,128,256]{3,2,1,0:T(8,128)S(1)} copy-done((f32[3,16,128,256]{3,2,1,0:T(8,128)S(1)}, f32[3,16,128,256]{3,2,1,0:T(8,128)}, u32[]{:S(2)}) %copy-start) | copy-done | bytes 6291480
  100.8 3.2 %edges.1 = (f32[16,8,256]{2,1,0:T(8,128)S(1)}, f32[16,8,256]{2,1,0:T(8,128)S(1)}, f32[16,8,128]{2,1,0:T(8,128)S(1)}, f32[16,8,128]{2,1,0:T(8,128)S(1)}) custom-call(f32[3,16,128,256]{3,2,1,0:T(8,128)S(1)} %copy-done), custom_call_target="tpu_custom_call" | custom-call | flops 1500000000 | bytes 5000000 | tf_op jit(solution)/shard_map/edges/pallas_call | solution.py:607
  106.6 2.1 collective-permute-start.3
  108.7 3.9 %x2.1 = f32[32,48,128]{2,1,0:T(8,128)S(1)} custom-call(s32[2]{0:T(128)S(1)} %pad_add_fusion.place_ref, f32[32,24,128]{2,1,0:T(8,128)} %all-to-all-done.3.in_ref, bf16[4,512,512]{2,1,0:T(8,128)(2,1)S(1)} %copy-done.8, bf16[4,512,512]{2,1,0:T(8,128)(2,1)S(1)} %copy-done.4), custom_call_target="tpu_custom_call" | custom-call | flops 1500000000 | bytes 5000000 | tf_op jit(solution)/shard_map/x2/pallas_call | solution.py:547
  113.5 27.9 %collective-permute-done.2.west_ref = f32[16,8,128]{2,1,0:T(8,128)S(1)} collective-permute-done((f32[16,8,128]{2,1,0:T(8,128)S(1)}, f32[16,8,128]{2,1,0:T(8,128)S(1)}, u32[]{:S(2)}, u32[]{:S(2)}) %collective-permute-start.2) | collective-permute-done | bytes 65568 | tf_op jit(solution)/shard_map/ppermute | solution.py:571
  143.3 10.6 %all-to-all-done.5.buf_ref = f32[32,144,128]{2,1,0:T(8,128)} async-done(((f32[32,144,128]{2,1,0:T(8,128)}), f32[32,144,128]{2,1,0:T(8,128)}, u32[]{:S(2)}, u32[]{:S(2)}) %all-to-all-start.5) | async-done | bytes 2359328 | tf_op jit(solution)/shard_map/all_to_all | solution.py:566
  153.9 5.8 %all-to-all-start.4 = ((f32[32,48,128]{2,1,0:T(8,128)}), f32[32,48,128]{2,1,0:T(8,128)S(1)}, u32[]{:S(2)}, u32[]{:S(2)}) async-start(f32[32,48,128]{2,1,0:T(8,128)} %copy-done.16), calls=%async_computation.4 | async-start | bytes 1572864 | tf_op jit(solution)/shard_map/all_to_all | solution.py:566
  160.7 8.0 %y6.1 = (f32[8,128,128]{2,1,0:T(8,128)S(1)}, f32[8,128,128]{2,1,0:T(8,128)S(1)}, f32[8,128,128]{2,1,0:T(8,128)S(1)}, f32[8,128,128]{2,1,0:T(8,128)S(1)}, f32[8,1...) custom-call(f32[32,144,128]{2,1,0:T(8,128)} %all-to-all-done.5.buf_ref, f32[8,128,128]{2,1,0:T(8,128)S(1)} %get-tuple-element.68.height_ref, ...), custom_call_target="tpu_custom_call" | custom-call | flops 2700000000 | bytes 9000000 | tf_op jit(solution)/shard_map/y6/pallas_call | solution.py:547
  172.8 7.5 %all-to-all-done.4.buf_ref = f32[32,48,128]{2,1,0:T(8,128)S(1)} async-done(((f32[32,48,128]{2,1,0:T(8,128)}), f32[32,48,128]{2,1,0:T(8,128)S(1)}, u32[]{:S(2)}, u32[]{:S(2)}) %all-to-all-start.4) | async-done | bytes 786464 | tf_op jit(solution)/shard_map/all_to_all | solution.py:566
  183.8 2.6 y2.1
  186.4 15.5 %all_to_all.50.in_ref = f32[32,24,128]{2,1,0:T(8,128)S(1)} all-to-all(f32[32,24,128]{2,1,0:T(8,128)S(1)} %get-tuple-element.78), channel_id=1, replica_groups=mesh['row'=8,'col'=4] {'row','col'}, dimensions={0} | all-to-all | bytes 786432 | tf_op jit(solution)/shard_map/all_to_all | solution.py:566
  201.9 2.9 %x1.3 = f32[32,24,128]{2,1,0:T(8,128)S(1)} custom-call(s32[2]{0:T(128)S(1)} %pad_add_fusion.place_ref, f32[32,24,128]{2,1,0:T(8,128)S(1)} %all_to_all.50.in_ref, bf16[4,512,512]{2,1,0:T(8,128)(2,1)S(1)} %copy-done.9, bf16[4,512,512]{2,1,0:T(8,128)(2,1)S(1)} %copy-done.5), custom_call_target="tpu_custom_call" | custom-call | flops 1200000000 | bytes 4000000 | tf_op jit(solution)/shard_map/x1/pallas_call | solution.py:547
  204.8 15.5 %all_to_all.51.buf_ref = f32[32,24,128]{2,1,0:T(8,128)S(1)} all-to-all(f32[32,24,128]{2,1,0:T(8,128)S(1)} %x1.3), channel_id=1, replica_groups=mesh['row'=8,'col'=4] {'row','col'}, dimensions={0} | all-to-all | bytes 786432 | tf_op jit(solution)/shard_map/all_to_all | solution.py:566
  220.3 3.4 %all-to-all-start.9 = ((f32[8,64,128]{2,1,0:T(8,128)}), f32[8,64,128]{2,1,0:T(8,128)S(1)}, u32[]{:S(2)}, u32[]{:S(2)}) async-start(f32[8,64,128]{2,1,0:T(8,128)} %get-tuple-element.87), calls=%async_computation.9 | async-start | bytes 524288 | tf_op jit(solution)/shard_map/all_to_all | solution.py:566
  227.8 2.4 y3.1
  230.3 3.9 %all-to-all-start.8 = ((f32[8,256,128]{2,1,0:T(8,128)}), f32[8,256,128]{2,1,0:T(8,128)S(1)}, u32[]{:S(2)}, u32[]{:S(2)}) async-start(f32[8,256,128]{2,1,0:T(8,128)} %y3.1), calls=%async_computation.8 | async-start | bytes 2097152 | tf_op jit(solution)/shard_map/all_to_all | solution.py:566
  235.2 2.8 %copy-done.1 = f32[3,16,128,256]{3,2,1,0:T(8,128)S(1)} copy-done((f32[3,16,128,256]{3,2,1,0:T(8,128)S(1)}, f32[3,16,128,256]{3,2,1,0:T(8,128)}, u32[]{:S(2)}) %copy-start.1) | copy-done | bytes 6291480
  238.0 14.5 %flow.1.flow_ref = f32[3,16,128,256]{3,2,1,0:T(8,128)} custom-call(f32[16,2]{1,0:T(8,128)S(1)} %copy.13.decay_ref, f32[3,16,128,256]{3,2,1,0:T(8,128)S(1)} %copy-done.1, f32[3,16,128,256]{3,2,1,0:T(8,128)S(1)} %copy-done.1, f32[3,16,128,256]{3,2,1,0:T(8,128)S(1)} %copy-done.1, f32[16,8,256]{2,1,0:T(8,128)S(1)} %collective-permute-done.south_ref, ...), custom_call_target="tpu_custom_call" | custom-call | flops 5699999744 | bytes 19000000 | tf_op jit(solution)/shard_map/flow/pallas_call | solution.py:661
  260.0 7.0 %load.1 = f32[3,16,128,256]{3,2,1,0:T(8,128)} custom-call(f32[16,2]{1,0:T(8,128)S(1)} %copy.13.decay_ref, f32[3,16,128,256]{3,2,1,0:T(8,128)} %flow.1.flow_ref, f32[128,256]{1,0:T(8,128)S(1)} %get-tuple-element.94.pressure_ref, f32[8,256]{1,0:T(8,128)S(1)} %collective-permute-done.4.south_ref, ...), custom_call_target="tpu_custom_call", output_to_operand_aliasing={{}: (1, {})} | custom-call | flops 1200000000 | bytes 4000000 | tf_op jit(solution)/shard_map/load/pallas_call | solution.py:691
  (129 shorter events, 49.5 us)
Async XLA Ops:
  4.0 18.4 %all-to-all-start = ((f32[8,256,128]{2,1,0:T(8,128)}), f32[8,256,128]{2,1,0:T(8,128)S(1)}, u32[]{:S(2)}, u32[]{:S(2)}) async-start(f32[8,256,128]{2,1,0:T(8,128)} %pack.1), calls=%async_computation | async-start | bytes 2097152 | tf_op jit(solution)/shard_map/all_to_all | solution.py:566
  10.2 13.9 %copy-start.10 = (bf16[8,192,512]{2,1,0:T(8,128)(2,1)}, bf16[8,192,512]{2,1,0:T(8,128)(2,1)S(1)}, u32[]{:S(2)}) copy-start(bf16[8,192,512]{2,1,0:T(8,128)(2,1)S(1)} %pad_maximum_fusion.4.yf) | copy-start | bytes 4718596
  25.0 26.0 %all-to-all-start.1 = ((f32[32,48,128]{2,1,0:T(8,128)}), f32[32,48,128]{2,1,0:T(8,128)S(1)}, u32[]{:S(2)}, u32[]{:S(2)}) async-start(f32[32,48,128]{2,1,0:T(8,128)} %copy-done.15), calls=%async_computation.1 | async-start | bytes 1572864 | tf_op jit(solution)/shard_map/all_to_all | solution.py:566
  35.4 20.1 %copy-start.2 = (bf16[4,512,512]{2,1,0:T(8,128)(2,1)}, bf16[4,512,512]{2,1,0:T(8,128)(2,1)S(1)}, u32[]{:S(2)}) copy-start(bf16[4,512,512]{2,1,0:T(8,128)(2,1)S(1)} %get-tuple-element.99.fl) | copy-start | bytes 6291460
  51.0 1.6 copy-start.6
  56.3 15.8 %all-to-all-start.2 = ((f32[32,24,128]{2,1,0:T(8,128)}), f32[32,24,128]{2,1,0:T(8,128)}, u32[]{:S(2)}, u32[]{:S(2)}) async-start(f32[32,24,128]{2,1,0:T(8,128)} %copy-done.14), calls=%async_computation.2 | async-start | bytes 786432 | tf_op jit(solution)/shard_map/all_to_all | solution.py:566
  72.1 1.4 copy-start.11
  78.3 15.8 %all-to-all-start.3 = ((f32[32,24,128]{2,1,0:T(8,128)}), f32[32,24,128]{2,1,0:T(8,128)}, u32[]{:S(2)}, u32[]{:S(2)}) async-start(f32[32,24,128]{2,1,0:T(8,128)} %copy-done.29), calls=%async_computation.3 | async-start | bytes 786432 | tf_op jit(solution)/shard_map/all_to_all | solution.py:566
  81.7 1.6 copy-start.3
  83.3 1.6 copy-start.7
  90.7 1.4 copy-start.13
  94.1 59.8 %all-to-all-start.5 = ((f32[32,144,128]{2,1,0:T(8,128)}), f32[32,144,128]{2,1,0:T(8,128)}, u32[]{:S(2)}, u32[]{:S(2)}) async-start(f32[32,144,128]{2,1,0:T(8,128)} %copy-done.13), calls=%async_computation.5 | async-start | bytes 4718592 | tf_op jit(solution)/shard_map/all_to_all | solution.py:566
  98.0 2.8 %copy-start = (f32[3,16,128,256]{3,2,1,0:T(8,128)S(1)}, f32[3,16,128,256]{3,2,1,0:T(8,128)}, u32[]{:S(2)}) copy-start(f32[3,16,128,256]{3,2,1,0:T(8,128)} %next_ref.1) | copy-start | bytes 18874372
  100.8 8.0 %copy-start.4 = (bf16[4,512,512]{2,1,0:T(8,128)(2,1)S(1)}, bf16[4,512,512]{2,1,0:T(8,128)(2,1)}, u32[]{:S(2)}) copy-start(bf16[4,512,512]{2,1,0:T(8,128)(2,1)} %copy-done.2) | copy-start | bytes 6291460
  100.8 8.0 %copy-start.8 = (bf16[4,512,512]{2,1,0:T(8,128)(2,1)S(1)}, bf16[4,512,512]{2,1,0:T(8,128)(2,1)}, u32[]{:S(2)}) copy-start(bf16[4,512,512]{2,1,0:T(8,128)(2,1)} %get-tuple-element.100.fh) | copy-start | bytes 6291460
  103.9 38.7 %collective-permute-start = (f32[16,8,256]{2,1,0:T(8,128)S(1)}, f32[16,8,256]{2,1,0:T(8,128)S(1)}, u32[]{:S(2)}, u32[]{:S(2)}) collective-permute-start(f32[16,8,256]{2,1,0:T(8,128)S(1)} %get-tuple-element.70), channel_id=1, source_target_pairs={{0,4},{4,8},{8,12},{12,16},{16,20},{20,24},{24,28},{28,0},{1,5},{5... | collective-permute-start | bytes 393224 | tf_op jit(solution)/shard_map/ppermute | solution.py:571
  105.5 37.2 %collective-permute-start.1 = (f32[16,8,256]{2,1,0:T(8,128)S(1)}, f32[16,8,256]{2,1,0:T(8,128)S(1)}, u32[]{:S(2)}, u32[]{:S(2)}) collective-permute-start(f32[16,8,256]{2,1,0:T(8,128)S(1)} %get-tuple-element.71), channel_id=1, source_target_pairs={{0,28},{4,0},{8,4},{12,8},{16,12},{20,16},{24,20},{28,24},{1,29},{... | collective-permute-start | bytes 393224 | tf_op jit(solution)/shard_map/ppermute | solution.py:571
  105.5 36.0 %collective-permute-start.2 = (f32[16,8,128]{2,1,0:T(8,128)S(1)}, f32[16,8,128]{2,1,0:T(8,128)S(1)}, u32[]{:S(2)}, u32[]{:S(2)}) collective-permute-start(f32[16,8,128]{2,1,0:T(8,128)S(1)} %get-tuple-element.72), channel_id=1, source_target_pairs={{0,1},{1,2},{2,3},{3,0},{4,5},{5,6},{6,7},{7,4},{8,9},{9,10},{10,1... | collective-permute-start | bytes 196616 | tf_op jit(solution)/shard_map/ppermute | solution.py:571
  106.6 35.4 %collective-permute-start.3 = (f32[16,8,128]{2,1,0:T(8,128)S(1)}, f32[16,8,128]{2,1,0:T(8,128)S(1)}, u32[]{:S(2)}, u32[]{:S(2)}) collective-permute-start(f32[16,8,128]{2,1,0:T(8,128)S(1)} %get-tuple-element.73), channel_id=1, source_target_pairs={{0,3},{1,0},{2,1},{3,2},{4,7},{5,4},{6,5},{7,6},{8,11},{9,8},{10,9... | collective-permute-start | bytes 196616 | tf_op jit(solution)/shard_map/ppermute | solution.py:571
  153.9 26.4 %all-to-all-start.4 = ((f32[32,48,128]{2,1,0:T(8,128)}), f32[32,48,128]{2,1,0:T(8,128)S(1)}, u32[]{:S(2)}, u32[]{:S(2)}) async-start(f32[32,48,128]{2,1,0:T(8,128)} %copy-done.16), calls=%async_computation.4 | async-start | bytes 1572864 | tf_op jit(solution)/shard_map/all_to_all | solution.py:566
  180.3 1.4 copy-start.12
  183.8 18.1 %copy-start.5 = (bf16[4,512,512]{2,1,0:T(8,128)(2,1)S(1)}, bf16[4,512,512]{2,1,0:T(8,128)(2,1)}, u32[]{:S(2)}) copy-start(bf16[4,512,512]{2,1,0:T(8,128)(2,1)} %copy-done.2) | copy-start | bytes 6291460
  183.8 18.1 %copy-start.9 = (bf16[4,512,512]{2,1,0:T(8,128)(2,1)S(1)}, bf16[4,512,512]{2,1,0:T(8,128)(2,1)}, u32[]{:S(2)}) copy-start(bf16[4,512,512]{2,1,0:T(8,128)(2,1)} %get-tuple-element.100.fh) | copy-start | bytes 6291460
  186.4 18.4 %copy-start.27 = (f32[8,128,128]{2,1,0:T(8,128)}, f32[8,128,128]{2,1,0:T(8,128)S(1)}, u32[]{:S(2)}) copy-start(f32[8,128,128]{2,1,0:T(8,128)S(1)} %get-tuple-element.79.vertical_in) | copy-start | bytes 1572868
  220.3 10.0 %all-to-all-start.9 = ((f32[8,64,128]{2,1,0:T(8,128)}), f32[8,64,128]{2,1,0:T(8,128)S(1)}, u32[]{:S(2)}, u32[]{:S(2)}) async-start(f32[8,64,128]{2,1,0:T(8,128)} %get-tuple-element.87), calls=%async_computation.9 | async-start | bytes 524288 | tf_op jit(solution)/shard_map/all_to_all | solution.py:566
  230.3 22.2 %all-to-all-start.8 = ((f32[8,256,128]{2,1,0:T(8,128)}), f32[8,256,128]{2,1,0:T(8,128)S(1)}, u32[]{:S(2)}, u32[]{:S(2)}) async-start(f32[8,256,128]{2,1,0:T(8,128)} %y3.1), calls=%async_computation.8 | async-start | bytes 2097152 | tf_op jit(solution)/shard_map/all_to_all | solution.py:566
  235.2 2.8 %copy-start.1 = (f32[3,16,128,256]{3,2,1,0:T(8,128)S(1)}, f32[3,16,128,256]{3,2,1,0:T(8,128)}, u32[]{:S(2)}) copy-start(f32[3,16,128,256]{3,2,1,0:T(8,128)} %next_ref.1) | copy-start | bytes 18874372
  238.0 14.5 %copy-start.38 = (f32[256,512]{1,0:T(8,128)S(1)}, f32[256,512]{1,0:T(8,128)}, u32[]{:S(2)}) copy-start(f32[256,512]{1,0:T(8,128)} %height_ref.3) | copy-start | bytes 1572868
  254.2 5.8 %collective-permute-start.4 = (f32[8,256]{1,0:T(8,128)S(1)}, f32[8,256]{1,0:T(8,128)S(1)}, u32[]{:S(2)}, u32[]{:S(2)}) collective-permute-start(f32[8,256]{1,0:T(8,128)S(1)} %get-tuple-element.95), channel_id=1, source_target_pairs={{0,4},{4,8},{8,12},{12,16},{16,20},{20,24},{24,28},{28,0},{1,5},{5... | collective-permute-start | bytes 24584 | tf_op jit(solution)/shard_map/ppermute | solution.py:571
  255.7 4.3 %collective-permute-start.5 = (f32[8,256]{1,0:T(8,128)S(1)}, f32[8,256]{1,0:T(8,128)S(1)}, u32[]{:S(2)}, u32[]{:S(2)}) collective-permute-start(f32[8,256]{1,0:T(8,128)S(1)} %get-tuple-element.96), channel_id=1, source_target_pairs={{0,28},{4,0},{8,4},{12,8},{16,12},{20,16},{24,20},{28,24},{1,29},{... | collective-permute-start | bytes 24584 | tf_op jit(solution)/shard_map/ppermute | solution.py:571
  255.7 4.3 %collective-permute-start.6 = (f32[8,128]{1,0:T(8,128)S(1)}, f32[8,128]{1,0:T(8,128)S(1)}, u32[]{:S(2)}, u32[]{:S(2)}) collective-permute-start(f32[8,128]{1,0:T(8,128)S(1)} %get-tuple-element.97), channel_id=1, source_target_pairs={{0,1},{1,2},{2,3},{3,0},{4,5},{5,6},{6,7},{7,4},{8,9},{9,10},{10,1... | collective-permute-start | bytes 12296 | tf_op jit(solution)/shard_map/ppermute | solution.py:571
  257.5 2.5 collective-permute-start.7
  (27 other events, 24.1 us)
